TPU v7x, 128 devices: a whole 4x4x4 slice. The times are simulated.
128 devices in a mesh: row: 8 (over x, core), col: 16 (over z, y).
Axes of the slice: x: 4, y: 4, z: 4, core: 2. Of those that a mesh axis runs over, the one named last changes fastest.
Arguments:
- fock_matrix: float32 [4096, 4096], P('row', 'col'), as said below
- density: float32 [4096, 4096], P('row', 'col'), as said below
- basis_gram: float32 [4096, 4096], P('row', 'col'), as said below
- error_history: float32 [6, 4096, 4096], P(None, 'row', 'col'), as said below
- fock_history: float32 [6, 4096, 4096], P(None, 'row', 'col'), may hold values from -6 to 6
Outputs:
- fock_next: float32 [4096, 4096], P('row', 'col')
- error_new: float32 [4096, 4096], P('row', 'col')
- weights: float32 [7], replicated
Inputs may be any that keep to these rules, and one draw needn't show every extreme that they name: `fock_matrix`: symmetric. `density`: symmetric. `basis_gram`: symmetric. `error_history`: each of the 6 matrices is antisymmetric.
All inputs are finite; a program needn't handle non-finite values.
Results may differ from a plain program's by a relative error of at most 0.000098.
Values sent between devices are 32-bit elements; how exact they have to be, the bound alone decides.
A program may use at most 128 MiB of HBM per device.

v0:
```python
import jax
import jax.numpy as jnp
from jax import lax
from jax.sharding import Mesh
from jax.sharding import PartitionSpec as P

ROW = ("row_0", "row_1")
COL = ("col_0", "col_1")


def from_everyone(shard, axis):
    devices = lax.axis_size(axis)
    return lax.all_to_all(
        jnp.broadcast_to(shard[None], (devices, *shard.shape)), axis, 0, 0, tiled=True
    )


def laid_out(parts, dim):
    lengths = list(parts.shape[1:])
    lengths[dim] *= parts.shape[0]
    return jnp.moveaxis(parts, 0, dim).reshape(lengths)


def gathered_by_axis(shard, axes, dim):
    far, near = axes
    parts = from_everyone(from_everyone(shard, far), near)
    return laid_out(parts.swapaxes(0, 1).reshape(-1, *shard.shape), dim)


def from_partner(value, axis, stride):
    mask = 2**stride
    pairs = [(source, source ^ mask) for source in range(lax.axis_size(axis))]
    return lax.ppermute(value, axis, pairs)


def over_copies(shard, axis):
    return from_everyone(shard, axis).sum(axis=0)


def by_axis(shard, axes):
    far, near = axes
    nearer = over_copies(shard, near)
    return over_copies(nearer, far)


def body(fock_matrix, density, basis_gram, error_history, fock_history):
    highest = lax.Precision.HIGHEST
    row_index = lax.axis_index(ROW)
    col_index = lax.axis_index(COL)
    dens_rows = lax.all_gather(density, COL, axis=1, tiled=True)
    gram_cols = gathered_by_axis(basis_gram, ("row_0", "row_1"), 0)
    middle = jnp.dot(dens_rows, gram_cols, precision=highest, preferred_element_type=jnp.float32)
    fock_rows = lax.all_gather(fock_matrix, COL, axis=1, tiled=True)
    middle_cols = gathered_by_axis(middle, ("row_0", "row_1"), 0)
    product = jnp.dot(fock_rows, middle_cols, precision=highest, preferred_element_type=jnp.float32)
    block_cols = product.shape[1]
    own_bit = col_index % 2
    upper_half = product[:block_cols]
    lower_half = product[block_cols:]
    keep_half = jnp.where(own_bit == 0, upper_half, lower_half)
    send_half = jnp.where(own_bit == 0, lower_half, upper_half)
    partner_half = from_partner(send_half, COL, 0)
    moving = jnp.where(
        own_bit == 0,
        jnp.concatenate([keep_half, partner_half], axis=1),
        jnp.concatenate([partner_half, keep_half], axis=1),
    )
    row_bits = lax.axis_size(ROW).bit_length() - 1
    for level in range(row_bits):
        row_bit = row_index // 2**level % 2
        col_bit = col_index // 2 ** (level + 1) % 2
        passing = from_partner(moving, ROW, level)
        arrived = from_partner(passing, COL, level + 1)
        moving = jnp.where(row_bit != col_bit, arrived, moving)
    flipped = moving.T
    error_new = product - flipped
    stacked = jnp.concatenate([error_history, error_new[None]], axis=0)
    gram_local = jnp.einsum("kij,lij->kl", stacked, stacked, precision=highest)
    gram = by_axis(gram_local, ("row_0", ("row_1", "col_0", "col_1")))
    size = gram.shape[0]
    factor = jnp.linalg.cholesky(gram)
    forward = []
    for index in range(size):
        total = jnp.float32(1.0)
        for inner in range(index):
            total = total - factor[index, inner] * forward[inner]
        forward.append(total / factor[index, index])
    backward = [None] * size
    for index in range(size - 1, -1, -1):
        total = forward[index]
        for inner in range(index + 1, size):
            total = total - factor[inner, index] * backward[inner]
        backward[index] = total / factor[index, index]
    solved = jnp.stack(backward)
    weights = solved / jnp.sum(solved)
    history_count = fock_history.shape[0]
    fock_next = (
        jnp.einsum("k,kij->ij", weights[:history_count], fock_history, precision=highest)
        + weights[history_count] * fock_matrix
    )
    return (fock_next, error_new, weights)


def solution(mesh):
    split = Mesh(mesh.devices.reshape(4, 2, 4, 4), ("row_0", "row_1", "col_0", "col_1"))
    placed = (P(ROW, COL), P(ROW, COL), P(ROW, COL), P(None, ROW, COL), P(None, ROW, COL))
    return jax.shard_map(
        body,
        mesh=split,
        in_specs=placed,
        out_specs=(P(ROW, COL), P(ROW, COL), P()),
        check_vma=False,
    )
```

profile of v0, /device:TPU:1, one launch (start us, length us, event | category | flops | bytes accessed | tf_op | source)
XLA Modules:
  0.0 364.6 jit_solution(14596943696388433436)
XLA Ops:
  9.9 30.1 %all_to_all.30 = f32[4,512,256]{2,1,0:T(8,128)S(1)} all-to-all(f32[4,512,256]{2,1,0:T(8,128)S(1)} %broadcast_in_dim.15), channel_id=1, replica_groups=mesh['row_0'=4,'row_1'=2,'col_0'=4,'col_1'=4] {'row_0'}, dimensions={0} | all-to-all | bytes 4194304 | tf_op jit(solution)/shard_map/all_to_all | solution.py:13
  40.3 8.5 %all_to_all.31 = f32[2,4,512,256]{3,2,1,0:T(8,128)S(1)} all-to-all(f32[2,4,512,256]{3,2,1,0:T(8,128)S(1)} %broadcast_in_dim.16), channel_id=1, replica_groups=mesh['row_0'=4,'row_1'=2,'col_0'=4,'col_1'=4] {'row_1'}, dimensions={0} | all-to-all | bytes 8388608 | tf_op jit(solution)/shard_map/all_to_all | solution.py:13
  51.1 38.2 %all-gather.3.cloned.1.call-done = f32[512,4096]{1,0:T(8,128)} async-done(((f32[512,256]{1,0:T(8,128)}), f32[512,4096]{1,0:T(8,128)}) %all-gather.3.cloned.1.call-update) | async-done | bytes 8388624 | tf_op jit(solution)/shard_map/all_gather | solution.py:50
  89.4 9.8 %fusion.16 = f32[512,256]{1,0:T(8,128)S(1)} fusion(f32[512,4096]{1,0:T(8,128)} %all-gather.3.cloned.1.call-done, f32[4096,256]{1,0:T(8,128)} %bitcast.63), kind=kOutput, calls=%fused_computation.29 | convolution fusion | flops 6442450944 | bytes 13107200 | tf_op jit(solution)/shard_map/dot_general | solution.py:52
  100.7 4.5 %all-to-all-start.2 = ((f32[4,512,256]{2,1,0:T(8,128)}), f32[4,512,256]{2,1,0:T(8,128)}, u32[]{:S(2)}, u32[]{:S(2)}) async-start(f32[4,512,256]{2,1,0:T(8,128)} %broadcast_in_dim.17), calls=%async_computation.2 | async-start | bytes 4194304 | tf_op jit(solution)/shard_map/all_to_all | solution.py:13
  105.2 24.4 %all-to-all-done.2 = f32[4,512,256]{2,1,0:T(8,128)} async-done(((f32[4,512,256]{2,1,0:T(8,128)}), f32[4,512,256]{2,1,0:T(8,128)}, u32[]{:S(2)}, u32[]{:S(2)}) %all-to-all-start.2) | async-done | bytes 2097184 | tf_op jit(solution)/shard_map/all_to_all | solution.py:13
  131.7 9.6 %all_to_all.32 = f32[2,4,512,256]{3,2,1,0:T(8,128)S(1)} all-to-all(f32[2,4,512,256]{3,2,1,0:T(8,128)S(1)} %broadcast_in_dim.18), channel_id=1, replica_groups=mesh['row_0'=4,'row_1'=2,'col_0'=4,'col_1'=4] {'row_1'}, dimensions={0} | all-to-all | bytes 8388608 | tf_op jit(solution)/shard_map/all_to_all | solution.py:13
  141.3 2.2 copy.37
  143.5 24.6 %all-gather.5.cloned.1.call-done = f32[512,4096]{1,0:T(8,128)} async-done(((f32[512,256]{1,0:T(8,128)}), f32[512,4096]{1,0:T(8,128)}) %all-gather.5.cloned.1.call-update) | async-done | bytes 8388624 | tf_op jit(solution)/shard_map/all_gather | solution.py:53
  168.1 16.5 %convolution_bitcast_fusion = f32[512,256]{0,1:T(8,128)S(1)} fusion(f32[4096,256]{1,0:T(8,128)} %bitcast.62, f32[512,4096]{1,0:T(8,128)} %all-gather.5.cloned.1.call-done), kind=kOutput, calls=%fused_computation.6 | convolution fusion | flops 6442450944 | bytes 13107200 | tf_op jit(solution)/shard_map/dot_general | solution.py:55
  191.1 4.9 %collective-permute-done = f32[256,256]{1,0:T(8,128)S(1)} collective-permute-done((f32[256,256]{1,0:T(8,128)S(1)}, f32[256,256]{1,0:T(8,128)S(1)}, u32[]{:S(2)}, u32[]{:S(2)}) %collective-permute-start) | collective-permute-done | bytes 262176 | tf_op jit(solution)/shard_map/ppermute | solution.py:33
  196.8 2.9 collective-permute-start.1
  203.2 13.1 %collective-permute-done.2 = f32[256,512]{1,0:T(8,128)} collective-permute-done((f32[256,512]{1,0:T(8,128)}, f32[256,512]{1,0:T(8,128)}, u32[]{:S(2)}, u32[]{:S(2)}) %collective-permute-start.2) | collective-permute-done | bytes 524320 | tf_op jit(solution)/shard_map/ppermute | solution.py:33
  219.4 11.2 %collective-permute-done.3 = f32[256,512]{1,0:T(8,128)} collective-permute-done((f32[256,512]{1,0:T(8,128)S(1)}, f32[256,512]{1,0:T(8,128)}, u32[]{:S(2)}, u32[]{:S(2)}) %collective-permute-start.3) | collective-permute-done | bytes 524320 | tf_op jit(solution)/shard_map/ppermute | solution.py:33
  231.5 10.8 %collective-permute-done.4 = f32[256,512]{1,0:T(8,128)} collective-permute-done((f32[256,512]{1,0:T(8,128)}, f32[256,512]{1,0:T(8,128)}, u32[]{:S(2)}, u32[]{:S(2)}) %collective-permute-start.4) | collective-permute-done | bytes 524320 | tf_op jit(solution)/shard_map/ppermute | solution.py:33
  244.2 2.7 collective-permute-start.5
  246.9 9.5 %collective-permute-done.5 = f32[256,512]{1,0:T(8,128)} collective-permute-done((f32[256,512]{1,0:T(8,128)S(1)}, f32[256,512]{1,0:T(8,128)}, u32[]{:S(2)}, u32[]{:S(2)}) %collective-permute-start.5) | collective-permute-done | bytes 524320 | tf_op jit(solution)/shard_map/ppermute | solution.py:33
  256.4 2.4 collective-permute-start.6
  258.8 5.7 %copy.40 = f32[6,512,256]{2,0,1:T(8,128)} copy(f32[6,512,256]{2,1,0:T(8,128)} %param.8) | data formatting | bytes 6291456 | tf_op args[3]
  264.5 3.4 collective-permute-done.6
  272.0 13.4 %fusion.6 = f32[7,7]{1,0:T(8,128)S(1)} fusion(f32[1,512,256]{2,0,1:T(1,128)} %copy.41, f32[6,512,256]{2,0,1:T(8,128)} %copy.40), kind=kOutput, calls=%fused_computation.7 | convolution fusion | flops 77987840 | bytes 3670212 | tf_op jit(solution)/shard_map/kij,lij->kl/dot_general | solution.py:78
  285.4 17.0 %all_to_all.33 = f32[32,7,7]{2,1,0:T(8,128)S(1)} all-to-all(f32[32,7,7]{2,1,0:T(8,128)S(1)} %broadcast_in_dim.20), channel_id=1, replica_groups=mesh['row_0'=4,'row_1'=2,'col_0'=4,'col_1'=4] {'row_1','col_0','col_1'}, dimensions={0} | all-to-all | bytes 12544 | tf_op jit(solution)/shard_map/all_to_all | solution.py:13
  303.0 4.0 %all-to-all-start.5 = ((f32[4,7,7]{2,1,0:T(8,128)}), f32[4,7,7]{2,1,0:T(8,128)S(1)}, u32[]{:S(2)}, u32[]{:S(2)}) async-start(f32[4,7,7]{2,1,0:T(8,128)} %broadcast_in_dim.21), calls=%async_computation.5 | async-start | bytes 32768 | tf_op jit(solution)/shard_map/all_to_all | solution.py:13
  351.1 5.2 %fusion.4 = f32[1,512,256]{2,0,1:T(1,128)S(1)} fusion(f32[6,512,256]{2,1,0:T(8,128)S(1)} %copy-done, f32[7]{0:T(128)S(1)} %broadcast_divide_fusion), kind=kOutput, calls=%fused_computation.4 | convolution fusion | flops 9437184 | bytes 3670044 | tf_op jit(solution)/shard_map/k,kij->ij/dot_general | solution.py:98
  (55 shorter events, 40.1 us)
Async XLA Ops:
  7.2 344.0 %copy-start = (f32[6,512,256]{2,1,0:T(8,128)S(1)}, f32[6,512,256]{2,1,0:T(8,128)}, u32[]{:S(2)}) copy-start(f32[6,512,256]{2,1,0:T(8,128)} %param.9) | copy-start | bytes 9437188
  7.2 82.2 %all-gather.3.cloned.1.call-start = ((), (), s32[]{:S(2)}) async-start(), calls=%async_computation.6 | async-start | bytes 8912896 | tf_op jit(solution)/shard_map/all_gather | solution.py:50
  7.9 160.2 %all-gather.5.cloned.1.call-start = ((), (), s32[]{:S(2)}) async-start(), calls=%async_computation.7 | async-start | bytes 8912896 | tf_op jit(solution)/shard_map/all_gather | solution.py:53
  100.7 29.0 %all-to-all-start.2 = ((f32[4,512,256]{2,1,0:T(8,128)}), f32[4,512,256]{2,1,0:T(8,128)}, u32[]{:S(2)}, u32[]{:S(2)}) async-start(f32[4,512,256]{2,1,0:T(8,128)} %broadcast_in_dim.17), calls=%async_computation.2 | async-start | bytes 4194304 | tf_op jit(solution)/shard_map/all_to_all | solution.py:13
  184.6 0.8 copy-start.1
  190.1 5.9 %collective-permute-start = (f32[256,256]{1,0:T(8,128)S(1)}, f32[256,256]{1,0:T(8,128)S(1)}, u32[]{:S(2)}, u32[]{:S(2)}) collective-permute-start(f32[256,256]{1,0:T(8,128)S(1)} %get-tuple-element.19), channel_id=1, source_target_pairs={{0,1},{1,0},{2,3},{3,2},{4,5},{5,4},{6,7},{7,6},{8,9},{9,8},{10,11... | collective-permute-start | bytes 786440 | tf_op jit(solution)/shard_map/ppermute | solution.py:33
  196.0 0.8 copy-start.5
  196.8 4.6 %collective-permute-start.1 = (f32[256,512]{1,0:T(8,128)S(1)}, f32[256,512]{1,0:T(8,128)}, u32[]{:S(2)}, u32[]{:S(2)}) collective-permute-start(f32[256,512]{1,0:T(8,128)S(1)} %maximum_select_fusion), channel_id=1, source_target_pairs={{0,16},{16,0},{32,48},{48,32},{64,80},{80,64},{96,112},{112,96},{1... | collective-permute-start | bytes 1572872 | tf_op jit(solution)/shard_map/ppermute | solution.py:33
  201.4 14.9 %collective-permute-start.2 = (f32[256,512]{1,0:T(8,128)}, f32[256,512]{1,0:T(8,128)}, u32[]{:S(2)}, u32[]{:S(2)}) collective-permute-start(f32[256,512]{1,0:T(8,128)} %collective-permute-done.1), channel_id=1, source_target_pairs={{0,2},{1,3},{2,0},{3,1},{4,6},{5,7},{6,4},{7,5},{8,10},{9,11},{10,... | collective-permute-start | bytes 1572872 | tf_op jit(solution)/shard_map/ppermute | solution.py:33
  217.4 0.8 copy-start.4
  218.2 12.4 %collective-permute-start.3 = (f32[256,512]{1,0:T(8,128)S(1)}, f32[256,512]{1,0:T(8,128)}, u32[]{:S(2)}, u32[]{:S(2)}) collective-permute-start(f32[256,512]{1,0:T(8,128)S(1)} %broadcast_select_fusion), channel_id=1, source_target_pairs={{0,32},{16,48},{32,0},{48,16},{64,96},{80,112},{96,64},{112,80},{1... | collective-permute-start | bytes 1572872 | tf_op jit(solution)/shard_map/ppermute | solution.py:33
  230.6 11.7 %collective-permute-start.4 = (f32[256,512]{1,0:T(8,128)}, f32[256,512]{1,0:T(8,128)}, u32[]{:S(2)}, u32[]{:S(2)}) collective-permute-start(f32[256,512]{1,0:T(8,128)} %collective-permute-done.3), channel_id=1, source_target_pairs={{0,4},{1,5},{2,6},{3,7},{4,0},{5,1},{6,2},{7,3},{8,12},{9,13},{10,... | collective-permute-start | bytes 1572872 | tf_op jit(solution)/shard_map/ppermute | solution.py:33
  243.4 0.8 copy-start.2
  244.2 12.2 %collective-permute-start.5 = (f32[256,512]{1,0:T(8,128)S(1)}, f32[256,512]{1,0:T(8,128)}, u32[]{:S(2)}, u32[]{:S(2)}) collective-permute-start(f32[256,512]{1,0:T(8,128)S(1)} %broadcast_select_fusion.1), channel_id=1, source_target_pairs={{0,64},{16,80},{32,96},{48,112},{64,0},{80,16},{96,32},{112,48},{1... | collective-permute-start | bytes 1572872 | tf_op jit(solution)/shard_map/ppermute | solution.py:33
  256.4 11.5 %collective-permute-start.6 = (f32[256,512]{1,0:T(8,128)}, f32[256,512]{1,0:T(8,128)}, u32[]{:S(2)}, u32[]{:S(2)}) collective-permute-start(f32[256,512]{1,0:T(8,128)} %collective-permute-done.5), channel_id=1, source_target_pairs={{0,8},{1,9},{2,10},{3,11},{4,12},{5,13},{6,14},{7,15},{8,0},{9,1},... | collective-permute-start | bytes 1572872 | tf_op jit(solution)/shard_map/ppermute | solution.py:33
  303.0 8.2 %all-to-all-start.5 = ((f32[4,7,7]{2,1,0:T(8,128)}), f32[4,7,7]{2,1,0:T(8,128)S(1)}, u32[]{:S(2)}, u32[]{:S(2)}) async-start(f32[4,7,7]{2,1,0:T(8,128)} %broadcast_in_dim.21), calls=%async_computation.5 | async-start | bytes 32768 | tf_op jit(solution)/shard_map/all_to_all | solution.py:13
  350.5 5.8 %copy-start.3 = (f32[512,256]{1,0:T(8,128)S(1)}, f32[512,256]{1,0:T(8,128)}, u32[]{:S(2)}) copy-start(f32[512,256]{1,0:T(8,128)} %param.5) | copy-start | bytes 1572868
  350.5 7.3 %copy-start.6 = (f32[7]{0:T(128)}, f32[7]{0:T(128)S(1)}, u32[]{:S(2)}) copy-start(f32[7]{0:T(128)S(1)} %broadcast_divide_fusion) | copy-start | bytes 88
Sparse Core Ops, SparseCore 0:
  10.1 79.2 all-gather.2
  91.5 76.6 all-gather.4
where the time goes:
time: 367 us; the launch traced here: 365 us
  waiting for transfers between devices  145 us (40%)
  blocking collectives  65.2 us (18%)
  between operations  50 us (14%)
  matrix products  44.8 us (12%)
  local copies, waits for them, and re-layouts  28.9 us (8%)
  starting transfers between devices  21.5 us (6%)
  other arithmetic  8.92 us (2%)
    all_to_all x4, blocking collectives, from_everyone(): lax.all_to_all(jnp.broadcast_to(shard[None], (devices, *shard.shape)), ax...  65.2 us
    ppermute x7, waiting for transfers between devices, from_partner(): return lax.ppermute(value, axis, pairs)  54.4 us
    all_gather x1, waiting for transfers between devices, body(): dens_rows = lax.all_gather(density, COL, axis=1, tiled=True)  38.2 us
    all_to_all x2, waiting for transfers between devices, from_everyone(): lax.all_to_all(jnp.broadcast_to(shard[None], (devices, *shard.shape)), ax...  26.6 us
    all_gather x1, waiting for transfers between devices, body(): fock_rows = lax.all_gather(fock_matrix, COL, axis=1, tiled=True)  24.6 us
    dot_general x1, matrix products, body(): jnp.dot(fock_rows, middle_cols, precision=highest, preferred_element_type...  16.5 us
    unnamed x18, local copies, waits for them, and re-layouts  13.8 us
    dot_general x1, matrix products, body(): gram_local = jnp.einsum('kij,lij->kl', stacked, stacked, precision=highest)  13.4 us
  transfers between devices with their start and end apart: 11, of which 11 were waited for; matrix products, arithmetic and copies ran while one was open for 7% of the time, Pallas kernels for 0%

commit v1 on v0

v1 whole, which is shorter than its diff:
```python
import jax
import jax.numpy as jnp
from jax import lax
from jax.experimental import pallas as pl
from jax.experimental.pallas import tpu as pltpu
from jax.sharding import Mesh
from jax.sharding import PartitionSpec as P

MESH = pl.DeviceIdType.MESH
F32 = jnp.float32
BF16 = jnp.bfloat16
UNITS = (((0, 0), (0, 1)), ((1, 0), (2, 1)), ((1, 1), (2, 0)), ((3, 0), (3, 1)))
NS, NU = 2, 4
NCOPY = 240
PAIRS = [(a, b) for a in range(6) for b in range(a, 6)]


def split(v):
    hi = v.astype(BF16)
    return hi, (v - hi.astype(F32)).astype(BF16)


def dot3(a_hi, a_lo, b_hi, b_lo):
    a = jnp.concatenate([a_hi, a_hi, a_lo], axis=1)
    b = jnp.concatenate([b_hi, b_lo, b_hi], axis=0)
    return jnp.dot(a, b, preferred_element_type=F32)


def kernel(
    f_hbm, d_hbm, s_hbm, eh_hbm, fh_hbm, next_hbm, err_hbm, w_ref,
    dg, sg, fg, dt_hi, dt_lo, s_hi, s_lo, f_hi, f_lo,
    mp, dx, ra, rb, fl, fr, mf, pacc, za, zb, zl, zr, pf, tb,
    eh, fh, err, out, red_y, red_z, red_x,
    send_sem, recv_sem, local_sem, t_send, t_recv,
):
    x, c, z, y = (lax.axis_index(n) for n in ("x", "c", "z", "y"))
    xr, xl, xo = lax.rem(x + 1, 4), lax.rem(x + 3, 4), lax.rem(x + 2, 4)
    dev = lambda x=x, c=c, z=z, y=y: (x, c, z, y)
    x_right, x_left = dev(x=xr), dev(x=xl)
    y_right, y_left = dev(y=lax.rem(y + 1, 4)), dev(y=lax.rem(y + 3, 4))
    z_right, z_left = dev(z=lax.rem(z + 1, 4)), dev(z=lax.rem(z + 3, 4))
    oc = 1 - c
    partner = dev(c=oc)

    sent = []

    def send(src, dst, to):
        k = len(sent)
        copy = pltpu.make_async_remote_copy(
            src_ref=src, dst_ref=dst, send_sem=send_sem.at[k], recv_sem=recv_sem.at[k],
            device_id=to, device_id_type=MESH,
        )
        copy.start()
        sent.append(copy)
        return copy

    local = []

    def load(src, dst):
        copy = pltpu.make_async_copy(src, dst, local_sem.at[len(local)])
        copy.start()
        local.append(copy)
        return copy

    def cols(ref, h):
        return ref.at[:, pl.ds(128 * h, 128)]

    load_d = [load(cols(d_hbm, h), dg.at[0, h]) for h in range(2)]
    load_s = [load(cols(s_hbm, h), sg.at[0, h]) for h in range(2)]
    load_f = [load(cols(f_hbm, h), fg.at[0, h]) for h in range(2)]
    load_e = load(eh_hbm, eh)
    load_h = load(fh_hbm, fh)

    barrier = pltpu.get_barrier_semaphore()
    for to in (x_right, x_left, y_right, y_left, z_right, z_left, partner):
        pl.semaphore_signal(barrier, inc=1, device_id=to, device_id_type=MESH)
    pl.semaphore_wait(barrier, 7)

    def y_sends(src, g):
        r0 = send(cols(src, 0), g.at[1, 0], y_right)
        l1 = send(cols(src, 1), g.at[2, 1], y_left)
        r1 = send(cols(src, 1), g.at[1, 1], y_right)
        l0 = send(cols(src, 0), g.at[2, 0], y_left)
        return r0, l1, r1, l0

    def y_forward(first, g):
        first[0].wait_recv()
        r = send(g.at[1, 0], g.at[3, 0], y_right)
        first[1].wait_recv()
        l = send(g.at[2, 1], g.at[3, 1], y_left)
        return r, l

    LO, HI = pl.ds(0, 256), pl.ds(256, 256)

    def z_sends(s):
        src = lambda rows: s_hbm.at[rows, pl.ds(128 * s, 128)]
        r0 = send(src(LO), sg.at[1, s, LO], z_right)
        l1 = send(src(HI), sg.at[2, s, HI], z_left)
        r1 = send(src(HI), sg.at[1, s, HI], z_right)
        l0 = send(src(LO), sg.at[2, s, LO], z_left)
        return r0, l1, r1, l0

    def z_forward(first, s):
        first[0].wait_recv()
        r = send(sg.at[1, s, LO], sg.at[3, s, LO], z_right)
        first[1].wait_recv()
        l = send(sg.at[2, s, HI], sg.at[3, s, HI], z_left)
        return r, l

    def prep_s(s, slots):
        for slot in slots:
            hi, lo = split(sg[slot, s])
            at = pl.ds(128 * slot, 128)
            s_hi[s, :, at] = hi
            s_lo[s, :, at] = lo

    def prep_d(u):
        for n, (slot, h) in enumerate(UNITS[u]):
            for k in range(4):
                hi, lo = split(dg[slot, h, pl.ds(128 * k, 128), :].T)
                dt_hi[u, pl.ds(128 * n, 128), pl.ds(128 * k, 128)] = hi
                dt_lo[u, pl.ds(128 * n, 128), pl.ds(128 * k, 128)] = lo

    def prep_f(u):
        for n, (slot, h) in enumerate(UNITS[u]):
            hi, lo = split(fg[slot, h])
            f_hi[u, :, pl.ds(128 * n, 128)] = hi
            f_lo[u, :, pl.ds(128 * n, 128)] = lo

    ALL, TOP, LOW = pl.ds(0, 32), pl.ds(0, 16), pl.ds(16, 16)
    g = [dict() for _ in range(NS * NU)]

    def p0(t):
        s, u = divmod(t, NU)
        tile = dot3(dt_hi[u], dt_lo[u], s_hi[s], s_lo[s])
        for k in range(2):
            for q in range(4):
                mp[t, k, q] = tile[(k * 4 + q) * 32 : (k * 4 + q + 1) * 32]
        g[t]["dx"] = send(mp.at[t, oc], dx.at[t], partner)

    def p1(t):
        g[t]["dx"].wait_recv()
        for q in range(4):
            mp[t, c, q] += dx[t, q]
        g[t]["ra"] = send(mp.at[t, c, xo, TOP], ra.at[t], x_right)
        g[t]["rb"] = send(mp.at[t, c, xo, LOW], rb.at[t], x_left)
        g[t]["fl1"] = send(mp.at[t, c, xr, LOW], fl.at[t, LOW], x_right)
        g[t]["fr0"] = send(mp.at[t, c, xl, TOP], fr.at[t, TOP], x_left)

    def p2(t):
        g[t]["ra"].wait_recv()
        mp[t, c, xr, TOP] += ra[t]
        g[t]["fl0"] = send(mp.at[t, c, xr, TOP], fl.at[t, TOP], x_right)
        g[t]["rb"].wait_recv()
        mp[t, c, xl, LOW] += rb[t]
        g[t]["fr1"] = send(mp.at[t, c, xl, LOW], fr.at[t, LOW], x_left)

    def p3(t):
        for name in ("fl1", "fr0", "fl0", "fr1"):
            g[t][name].wait_recv()
        mf[t, c, x] = mp[t, c, x] + fl[t] + fr[t]
        top, low = mf.at[t, c, x, TOP], mf.at[t, c, x, LOW]
        g[t]["gr0"] = send(top, top, x_right)
        g[t]["gl1"] = send(low, low, x_left)
        g[t]["gr1"] = send(low, low, x_right)
        g[t]["gl0"] = send(top, top, x_left)
        g[t]["gp"] = send(mf.at[t, c, x], mf.at[t, c, x], partner)

    def p4(t):
        g[t]["gr0"].wait_recv()
        g[t]["hr"] = send(mf.at[t, c, xl, TOP], mf.at[t, c, xl, TOP], x_right)
        g[t]["gl1"].wait_recv()
        g[t]["hl"] = send(mf.at[t, c, xr, LOW], mf.at[t, c, xr, LOW], x_left)
        g[t]["gr1"].wait_recv()
        g[t]["ql"] = send(mf.at[t, c, xl], mf.at[t, c, xl], partner)
        g[t]["gl0"].wait_recv()
        g[t]["qr"] = send(mf.at[t, c, xr], mf.at[t, c, xr], partner)

    def p5(t):
        g[t]["hr"].wait_recv()
        g[t]["hl"].wait_recv()
        g[t]["qo"] = send(mf.at[t, c, xo], mf.at[t, c, xo], partner)

    def p6(t):
        s, u = divmod(t, NU)
        for name in ("gp", "ql", "qr", "qo"):
            g[t][name].wait_recv()
        m_hi, m_lo = split(jnp.concatenate([mf[t, k, q] for k in range(2) for q in range(4)], axis=0))
        part = dot3(f_hi[u], f_lo[u], m_hi, m_lo)
        for slot in range(4):
            piece = part[:, 128 * slot : 128 * (slot + 1)]
            if u == 0:
                pacc[s, slot] = piece
            else:
                pacc[s, slot] += piece

    w = [dict() for _ in range(NS)]

    def z1(s):
        w[s]["za"] = send(pacc.at[s, 3, LO], za.at[s], z_right)
        w[s]["zb"] = send(pacc.at[s, 3, HI], zb.at[s], z_left)
        w[s]["zl1"] = send(pacc.at[s, 2, HI], zl.at[s, HI], z_right)
        w[s]["zr0"] = send(pacc.at[s, 1, LO], zr.at[s, LO], z_left)

    def z2(s):
        w[s]["za"].wait_recv()
        pacc[s, 2, LO] += za[s]
        w[s]["zl0"] = send(pacc.at[s, 2, LO], zl.at[s, LO], z_right)
        w[s]["zb"].wait_recv()
        pacc[s, 1, HI] += zb[s]
        w[s]["zr1"] = send(pacc.at[s, 1, HI], zr.at[s, HI], z_left)

    own_half = lax.rem(y, 2)
    t_core = lax.div(y, 2)
    mirror = jnp.logical_and(x == z, c == t_core)

    def t_copy(s, h):
        return pltpu.make_async_remote_copy(
            src_ref=pf.at[s, pl.ds(256 * h, 256)], dst_ref=tb.at[own_half, s],
            send_sem=t_send.at[s, h], recv_sem=t_recv.at[s, own_half],
            device_id=(z, t_core, x, 2 * c + h), device_id_type=MESH,
        )

    def t_local(s, h):
        return pltpu.make_async_copy(pf.at[s, pl.ds(256 * h, 256)], tb.at[own_half, s], t_recv.at[s, own_half])

    def z3(s):
        for name in ("zl1", "zr0", "zl0", "zr1"):
            w[s][name].wait_recv()
        pf[s] = pacc[s, 0] + zl[s] + zr[s]
        for h in range(2):
            mine = jnp.logical_and(mirror, own_half == h)

            @pl.when(mine)
            def _():
                t_local(s, h).start()

            @pl.when(jnp.logical_not(mine))
            def _():
                t_copy(s, h).start()

    def t_wait(s, half):
        pltpu.make_async_copy(pf.at[s, LO], tb.at[half, s], t_recv.at[s, half]).wait()

    def history_gram():
        def step(n, acc):
            rows = pl.ds(pl.multiple_of(8 * n, 8), 8)
            acc = list(acc)
            for col in range(2):
                e = [eh[k, rows, pl.ds(128 * col, 128)] for k in range(6)]
                acc = [v + e[a] * e[b] for v, (a, b) in zip(acc, PAIRS)]
            return tuple(acc)

        acc = lax.fori_loop(0, 64, step, tuple(jnp.zeros((8, 128), F32) for _ in PAIRS))
        return [jnp.sum(v, axis=0, keepdims=True) for v in acc]

    d_first = y_sends(d_hbm, dg)
    s_first = [z_sends(0)]
    for n in load_d + load_s:
        n.wait()
    prep_d(0)
    for s in range(NS):
        prep_s(s, (0,))
    load_e.wait()
    hist = history_gram()
    s_fwd = [z_forward(s_first[0], 0)]
    s_first.append(z_sends(1))
    d_fwd = y_forward(d_first, dg)
    f_first = y_sends(f_hbm, fg)
    prep_d(1)
    s_first[0][2].wait_recv()
    s_first[0][3].wait_recv()
    prep_s(0, (1, 2))
    s_fwd[0][0].wait_recv()
    s_fwd[0][1].wait_recv()
    prep_s(0, (3,))
    p0(0)
    p0(1)
    p1(0)
    p1(1)
    s_fwd.append(z_forward(s_first[1], 1))
    d_first[2].wait_recv()
    d_first[3].wait_recv()
    prep_d(2)
    p0(2)
    p2(0)
    p2(1)
    p1(2)
    p3(0)
    p3(1)
    d_fwd[0].wait_recv()
    d_fwd[1].wait_recv()
    prep_d(3)
    p0(3)
    p2(2)
    p1(3)
    p4(0)
    s_first[1][2].wait_recv()
    s_first[1][3].wait_recv()
    prep_s(1, (1, 2))
    s_fwd[1][0].wait_recv()
    s_fwd[1][1].wait_recv()
    prep_s(1, (3,))
    p0(4)
    p4(1)
    p3(2)
    p2(3)
    p1(4)
    f_fwd = y_forward(f_first, fg)
    for n in load_f:
        n.wait()
    prep_f(0)
    p0(5)
    p5(0)
    p5(1)
    p6(0)
    p4(2)
    p3(3)
    p2(4)
    p1(5)
    prep_f(1)
    p0(6)
    p6(1)
    p5(2)
    p4(3)
    p3(4)
    p2(5)
    p1(6)
    f_first[2].wait_recv()
    f_first[3].wait_recv()
    prep_f(2)
    p0(7)
    p6(2)
    p5(3)
    p4(4)
    p3(5)
    p2(6)
    p1(7)
    f_fwd[0].wait_recv()
    f_fwd[1].wait_recv()
    prep_f(3)
    p6(3)
    z1(0)
    p5(4)
    p4(5)
    p3(6)
    p2(7)
    p6(4)
    p5(5)
    p4(6)
    p3(7)
    z2(0)
    p6(5)
    p5(6)
    p4(7)
    p6(6)
    p5(7)
    p6(7)
    z1(1)
    z3(0)
    z2(1)
    z3(1)

    sums = [jnp.zeros((8, 128), F32) for _ in range(7)]
    load_h.wait()
    for half in range(2):
        for s in range(NS):
            t_wait(s, half)
            start = 256 * half + 128 * s
            rows = pl.ds(start, 128)
            for col in range(2):
                at = pl.ds(128 * col, 128)
                err[rows, at] = pf[col, rows, :] - tb[half, s, at, :].T

            def step(n, acc):
                at = pl.ds(pl.multiple_of(start + 8 * n, 8), 8)
                for col in range(2):
                    lanes = pl.ds(128 * col, 128)
                    e = err[at, lanes]
                    acc = tuple(acc[k] + eh[k, at, lanes] * e for k in range(6)) + (acc[6] + e * e,)
                return acc

            sums = lax.fori_loop(0, 16, step, tuple(sums))
    err_out = load(err, err_hbm)

    top = hist + [jnp.sum(v, axis=0, keepdims=True) for v in sums] + [jnp.zeros((4, 128), F32)]
    red_y[y] = jnp.concatenate(top, axis=0)
    for d in range(1, 4):
        send(red_y.at[y], red_y.at[y], dev(y=lax.rem(y + d, 4)))
    for copy in sent[-3:]:
        copy.wait_recv()
    red_z[z] = red_y[0] + red_y[1] + red_y[2] + red_y[3]
    for d in range(1, 4):
        send(red_z.at[z], red_z.at[z], dev(z=lax.rem(z + d, 4)))
    for copy in sent[-3:]:
        copy.wait_recv()
    me = 2 * x + c
    red_x[me] = red_z[0] + red_z[1] + red_z[2] + red_z[3]
    for d in range(1, 8):
        to = lax.rem(me + d, 8)
        send(red_x.at[me], red_x.at[me], dev(x=lax.div(to, 2), c=lax.rem(to, 2)))
    for copy in sent[-7:]:
        copy.wait_recv()
    total = red_x[0]
    for k in range(1, 8):
        total = total + red_x[k]
    total = jnp.broadcast_to(jnp.sum(total, axis=1, keepdims=True), (32, 128))

    gram = {}
    for n, (a, b) in enumerate(PAIRS):
        gram[b, a] = total[n : n + 1]
    for k in range(7):
        gram[6, k] = total[21 + k : 22 + k]
    low = {}
    for j in range(7):
        v = gram[j, j]
        for k in range(j):
            v = v - low[j, k] * low[j, k]
        low[j, j] = jnp.sqrt(v)
        for i in range(j + 1, 7):
            v = gram[i, j]
            for k in range(j):
                v = v - low[i, k] * low[j, k]
            low[i, j] = v / low[j, j]
    forward = []
    for i in range(7):
        v = jnp.ones((1, 128), F32)
        for k in range(i):
            v = v - low[i, k] * forward[k]
        forward.append(v / low[i, i])
    backward = [None] * 7
    for i in range(6, -1, -1):
        v = forward[i]
        for k in range(i + 1, 7):
            v = v - low[k, i] * backward[k]
        backward[i] = v / low[i, i]
    norm = backward[0]
    for v in backward[1:]:
        norm = norm + v
    weights = [v / norm for v in backward]
    lane = lax.broadcasted_iota(jnp.int32, (1, 128), 1)
    row = jnp.zeros((1, 128), F32)
    for k in range(7):
        row = jnp.where(lane == k, weights[k], row)
    w_ref[...] = row
    spread = [jnp.broadcast_to(v, (8, 128)) for v in weights]

    def mix(n, carry):
        at = pl.ds(pl.multiple_of(8 * n, 8), 8)
        for col in range(2):
            lanes = pl.ds(128 * col, 128)
            v = spread[6] * fg[0, col, at, :]
            for k in range(6):
                v = v + spread[k] * fh[k, at, lanes]
            out[at, lanes] = v
        return carry

    lax.fori_loop(0, 64, mix, 0)
    next_out = load(out, next_hbm)
    for copy in sent:
        copy.wait_send()
    for s in range(NS):
        for h in range(2):

            @pl.when(jnp.logical_not(jnp.logical_and(mirror, own_half == h)))
            def _():
                t_copy(s, h).wait_send()

    err_out.wait()
    next_out.wait()


def body(fock_matrix, density, basis_gram, error_history, fock_history):
    any_ = pl.BlockSpec(memory_space=pl.ANY)
    v = pltpu.VMEM
    block = jax.ShapeDtypeStruct((512, 256), F32)
    next_, err, w = pl.pallas_call(
        kernel,
        out_shape=(block, block, jax.ShapeDtypeStruct((1, 128), F32)),
        in_specs=[any_] * 5,
        out_specs=(any_, any_, pl.BlockSpec(memory_space=pltpu.VMEM)),
        scratch_shapes=[
            v((4, 2, 512, 128), F32), v((4, 2, 512, 128), F32), v((4, 2, 512, 128), F32),
            v((4, 256, 512), BF16), v((4, 256, 512), BF16),
            v((2, 512, 512), BF16), v((2, 512, 512), BF16),
            v((4, 512, 256), BF16), v((4, 512, 256), BF16),
            v((8, 2, 4, 32, 512), F32), v((8, 4, 32, 512), F32),
            v((8, 16, 512), F32), v((8, 16, 512), F32),
            v((8, 32, 512), F32), v((8, 32, 512), F32),
            v((8, 2, 4, 32, 512), F32),
            v((2, 4, 512, 128), F32),
            v((2, 256, 128), F32), v((2, 256, 128), F32),
            v((2, 512, 128), F32), v((2, 512, 128), F32),
            v((2, 512, 128), F32),
            v((2, 2, 256, 128), F32),
            v((6, 512, 256), F32), v((6, 512, 256), F32),
            v((512, 256), F32), v((512, 256), F32),
            v((4, 32, 128), F32), v((4, 32, 128), F32), v((8, 32, 128), F32),
            pltpu.SemaphoreType.DMA((NCOPY,)), pltpu.SemaphoreType.DMA((NCOPY,)),
            pltpu.SemaphoreType.DMA((10,)),
            pltpu.SemaphoreType.DMA((2, 2)), pltpu.SemaphoreType.DMA((2, 2)),
        ],
        compiler_params=pltpu.CompilerParams(
            collective_id=0, has_side_effects=True, vmem_limit_bytes=60 * 1024 * 1024
        ),
    )(fock_matrix, density, basis_gram, error_history, fock_history)
    return next_, err, w[0, :7]


def solution(mesh):
    split_mesh = Mesh(mesh.devices.reshape(4, 2, 4, 4), ("x", "c", "z", "y"))
    two = P(("x", "c"), ("z", "y"))
    three = P(None, ("x", "c"), ("z", "y"))
    return jax.shard_map(
        body,
        mesh=split_mesh,
        in_specs=(two, two, two, three, three),
        out_specs=(two, two, P()),
        check_vma=False,
    )
```

time: 367 us -> 127 us (0.35)
  waiting for transfers between devices: 145 us -> 0 us
  Pallas kernels: 0 us -> 121 us
  blocking collectives: 65.2 us -> 0 us
  between operations: 50 us -> 0.64 us
  matrix products: 44.8 us -> 0 us
  local copies, waits for them, and re-layouts: 28.9 us -> 4.85 us
  starting transfers between devices: 21.5 us -> 0 us
  other arithmetic: 8.92 us -> 0 us
    pallas_call x0 -> x1, Pallas kernels: none -> 121 us  [body(): pl.pallas_call(kernel, out_shape=(block, block, jax.ShapeDtypeStruct((1,...]
    all_to_all x4 -> x0, blocking collectives: 65.2 us -> none  [from_everyone(): lax.all_to_all(jnp.broadcast_to(shard[None], (devices, *shard.shape)), ax...]
    all_gather x2 -> x0, waiting for transfers between devices: 62.8 us -> none  [the longest x1 38.2 us: body(): dens_rows = lax.all_gather(density, COL, axis=1, tiled=True)]
    ppermute x7 -> x0, waiting for transfers between devices: 54.4 us -> none  [from_partner(): return lax.ppermute(value, axis, pairs)]
    dot_general x4 -> x0, matrix products: 44.8 us -> none  [the longest x1 16.5 us: body(): jnp.dot(fock_rows, middle_cols, precision=highest, preferred_element_type...]
    all_to_all x2 -> x0, waiting for transfers between devices: 26.6 us -> none  [from_everyone(): lax.all_to_all(jnp.broadcast_to(shard[None], (devices, *shard.shape)), ax...]
    ppermute x7 -> x0, starting transfers between devices: 12.9 us -> none  [from_partner(): return lax.ppermute(value, axis, pairs)]
    unnamed x18 -> x2, local copies, waits for them, and re-layouts: 13.8 us -> 3.73 us
  transfers between devices with their start and end apart: 11 -> 0, of which waited for: 11 -> 0; matrix products, arithmetic and copies ran while one was open for 7% -> 0% of each run, Pallas kernels for 0% -> 0%
where the time goes in v1:
time: 127 us
  Pallas kernels  121 us (95%)
  local copies, waits for them, and re-layouts  4.85 us (4%)
    pallas_call x1, Pallas kernels, body(): pl.pallas_call(kernel, out_shape=(block, block, jax.ShapeDtypeStruct((1,...  121 us
    unnamed x2, local copies, waits for them, and re-layouts  3.73 us

profile of v1, /device:TPU:1, one launch (start us, length us, event | category | flops | bytes accessed | tf_op | source)
XLA Modules:
  0.0 126.8 jit_solution(338282570344238360)
XLA Ops:
  0.6 121.3 %shard_map.76 = (f32[512,256]{1,0:T(8,128)}, f32[512,256]{1,0:T(8,128)}, f32[1,128]{1,0:T(1,128)}) custom-call(f32[512,256]{1,0:T(8,128)} %f_hbm.1, f32[512,256]{1,0:T(8,128)} %d_hbm.1, f32[512,256]{1,0:T(8,128)} %s_hbm.1, f32[6,512,256]{2,1,0:T(8,128)} %eh_hbm.1, f32[6,512,256]{2,1,0:T(8,128)} %fh_hbm.1), custom_call_target="tpu_custom_call" | custom-call | tf_op jit(solution)/shard_map/pallas_call | solution.py:477
  121.9 1.1 slice_bitcast_fusion
  123.1 1.9 %copy.10 = f32[512,256]{1,0:T(8,128)} copy(f32[512,256]{1,0:T(8,128)} %get-tuple-element.12) | data formatting | bytes 1048576
  124.9 1.9 %copy.11 = f32[512,256]{1,0:T(8,128)} copy(f32[512,256]{1,0:T(8,128)} %get-tuple-element.13) | data formatting | bytes 1048576

commit v2 on v0

v2 whole, which is shorter than its diff:
```python
import jax
import jax.numpy as jnp
from jax import lax
from jax.experimental import pallas as pl
from jax.experimental.pallas import tpu as pltpu
from jax.sharding import Mesh
from jax.sharding import PartitionSpec as P

MESH = pl.DeviceIdType.MESH
F32 = jnp.float32
BF16 = jnp.bfloat16
UNITS = (((0, 0), (0, 1)), ((1, 0), (2, 1)), ((1, 1), (2, 0)), ((3, 0), (3, 1)))
NS, NU = 4, 4
PAIRS = [(a, b) for a in range(6) for b in range(a, 6)]
GROUPS = (
    (0, 0, 1),
    (0, 1, 1),
    (1, 0, 2),
    (0, 2, 1),
    (1, 2, 1),
    (2, 0, 2),
    (0, 3, 1),
    (1, 3, 1),
    (2, 2, 2),
    (3, 0, 2),
    (3, 2, 2),
)
ORDER = (
    ("ys", 0), ("zs", 0), ("pd", 0), ("hist", 0), ("zf", 0), ("zs", 1), ("ps", 0), ("p0", 0), ("zf", 1), ("zs", 2),
    ("yf", 0), ("fs", 0), ("pd", 1), ("p0", 1), ("p1", 0), ("pf", 0, 0), ("pf", 0, 1), ("p1", 1), ("p2", 0),
    ("ps", 1), ("p0", 2), ("p2", 1), ("zf", 2), ("zs", 3), ("pd", 2), ("p0", 3), ("p1", 2), ("p0", 4), ("p3", 0),
    ("p1", 3), ("p3", 1), ("p1", 4), ("ps", 2), ("p0", 5), ("p2", 2), ("pd", 3), ("p0", 6), ("zf", 3), ("p0", 7),
    ("p4", 0), ("p1", 5), ("p2", 3), ("p0", 8), ("p1", 6), ("p4", 1), ("p1", 7), ("p2", 4), ("p3", 2), ("ff", 0),
    ("fs", 1), ("p1", 8), ("p5", 0), ("pf", 1, 0), ("ps", 3), ("p0", 9), ("p6", 0, 0), ("p6", 0, 1), ("p2", 5),
    ("p2", 6), ("p0", 10), ("p5", 1), ("p1", 9), ("p2", 7), ("pf", 2, 0), ("p3", 3), ("p3", 4), ("p1", 10),
    ("p6", 1, 0), ("pf", 3, 0), ("p4", 2), ("p2", 8), ("p3", 5), ("p3", 6), ("p2", 9), ("ff", 1), ("pf", 1, 1),
    ("p6", 1, 1), ("p3", 7), ("p4", 3), ("p4", 4), ("p2", 10), ("pf", 2, 1), ("p5", 2), ("p3", 8), ("p6", 2, 0),
    ("p6", 2, 1), ("p4", 5), ("pf", 3, 1), ("p4", 6), ("p3", 9), ("p4", 7), ("p5", 3), ("p5", 4), ("p3", 10),
    ("p6", 3, 0), ("p6", 3, 1), ("p6", 4, 0), ("p6", 4, 1), ("p4", 8), ("p5", 5), ("p5", 6), ("p6", 5, 0),
    ("p6", 5, 1), ("p4", 9), ("p5", 7), ("p6", 6, 0), ("p6", 6, 1), ("z1", 0, 0), ("z1", 0, 1), ("p4", 10),
    ("p6", 7, 0), ("p6", 7, 1), ("p5", 8), ("z1", 1, 0), ("z1", 1, 1), ("p5", 9), ("p6", 8, 0), ("p6", 8, 1),
    ("z2", 0, 0), ("p6", 9, 0), ("p5", 10), ("p6", 9, 1), ("z2", 0, 1), ("z1", 2, 0), ("z1", 2, 1), ("p6", 10, 0),
    ("p6", 10, 1), ("z2", 1, 0), ("z1", 3, 0), ("z1", 3, 1), ("z2", 1, 1), ("z3", 0, 0), ("ha",), ("z3", 0, 1),
    ("z2", 2, 0), ("z2", 2, 1), ("z3", 1, 0), ("z2", 3, 0), ("z2", 3, 1), ("z3", 1, 1), ("t", 0, 0), ("t", 0, 1),
    ("z3", 2, 0), ("hb",), ("z3", 2, 1), ("z3", 3, 0), ("z3", 3, 1), ("hc",), ("t", 2, 0), ("t", 2, 1),
)
N_RECV = 49 + 9 * len(GROUPS)
RELAYED = (0, 2)
RELAY_AXIS = "z"


def split(v):
    hi = v.astype(BF16)
    return hi, (v - hi.astype(F32)).astype(BF16)


def dot3(a_hi, a_lo, b_hi, b_lo):
    a = jnp.concatenate([a_hi, a_hi, a_lo], axis=1)
    b = jnp.concatenate([b_hi, b_lo, b_hi], axis=0)
    return jnp.dot(a, b, preferred_element_type=F32)


def kernel(
    f_hbm, d_hbm, s_hbm, eh_hbm, fh_hbm, next_hbm, err_hbm, w_ref,
    s_in, sg, dg, fg, s_hi, s_lo, d_hi, d_lo, f_hi, f_lo,
    mp, dx, ra, rb, flr, mf, m_hi, m_lo, pacc, za, zb, zlr, pf, tb, hop,
    eh, fh, own, err, out, ha, hb, na, nb,
    send_sem, recv_sem, local_sem, t_send, t_recv, hop_recv, hop_send,
):
    x, c, z, y = (lax.axis_index(n) for n in ("x", "c", "z", "y"))
    xr, xl, xo = lax.rem(x + 1, 4), lax.rem(x + 3, 4), lax.rem(x + 2, 4)
    dev = lambda x=x, c=c, z=z, y=y: (x, c, z, y)
    x_right, x_left = dev(x=xr), dev(x=xl)
    y_right, y_left = dev(y=lax.rem(y + 1, 4)), dev(y=lax.rem(y + 3, 4))
    z_right, z_left = dev(z=lax.rem(z + 1, 4)), dev(z=lax.rem(z + 3, 4))
    oc = 1 - c
    partner = dev(c=oc)

    used = {"send": 0, "recv": 0}
    outgoing = []

    def recv():
        used["recv"] += 1
        return recv_sem.at[used["recv"] - 1]

    def sender(*whole):
        used["send"] += len(whole)
        base = used["send"] - len(whole)
        for k, ref in enumerate(whole):
            outgoing.append((send_sem.at[base + k], ref))
        return [send_sem.at[base + k] for k in range(len(whole))]

    def send(src, dst, to, out_sem, in_sem):
        pltpu.make_async_remote_copy(
            src_ref=src, dst_ref=dst, send_sem=out_sem, recv_sem=in_sem, device_id=to, device_id_type=MESH,
        ).start()

    def wait(sem, ref):
        pltpu.make_async_copy(ref, ref, sem).wait()

    local = []

    def load(src, dst):
        copy = pltpu.make_async_copy(src, dst, local_sem.at[len(local)])
        copy.start()
        local.append(copy)
        return copy

    lanes = [pl.ds(0, 128), pl.ds(128, 128)]
    halves = [pl.ds(0, 256), pl.ds(256, 256)]

    barrier = pltpu.get_barrier_semaphore()
    for to in (x_right, x_left, y_right, y_left, z_right, z_left, partner):
        pl.semaphore_signal(barrier, inc=1, device_id=to, device_id_type=MESH)
    load_s = load(s_hbm, s_in)
    load_d = [load(d_hbm.at[:, lanes[h]], dg.at[0, h]) for h in range(2)]
    load_e = load(eh_hbm, eh)
    load_f = [load(f_hbm.at[halves[r], lanes[h]], fg.at[0, r, h]) for r in range(2) for h in range(2)]
    load_h = load(fh_hbm, fh)
    load_s.wait()
    for n in range(2):
        for k in range(4):
            block = s_in[pl.ds(128 * k, 128), lanes[n]].T
            for e in range(2):
                sg[0, 2 * n + e, :, pl.ds(128 * k, 128)] = block[64 * e : 64 * (e + 1)]
    pl.semaphore_wait(barrier, 7)

    three = pl.ds(0, 3)
    (d_out,) = sender(dg.at[three])
    (f_out,) = sender(fg.at[three])
    (s_out,) = sender(sg.at[three])

    class Line:
        def __init__(self, src, slot, size, right, left, out_sem):
            self.src, self.slot, self.size, self.right, self.left, self.out = src, slot, size, right, left, out_sem
            self.sems = [recv() for _ in range(3)]

        def begin(self):
            a, b, _ = self.sems
            send(self.src(0), self.slot(1, 0), self.right, self.out, a)
            send(self.src(1), self.slot(2, 1), self.left, self.out, a)
            send(self.src(1), self.slot(1, 1), self.right, self.out, b)
            send(self.src(0), self.slot(2, 0), self.left, self.out, b)

        def forward(self):
            wait(self.sems[0], self.size)
            send(self.slot(1, 0), self.slot(3, 0), self.right, self.out, self.sems[2])
            send(self.slot(2, 1), self.slot(3, 1), self.left, self.out, self.sems[2])

        def second(self):
            wait(self.sems[1], self.size)

        def third(self):
            wait(self.sems[2], self.size)

    d_line = Line(lambda h: d_hbm.at[:, lanes[h]], lambda slot, h: dg.at[slot, h], dg.at[1], y_right, y_left, d_out)
    f_line = [
        Line(
            lambda h, r=r: f_hbm.at[halves[r], lanes[h]], lambda slot, h, r=r: fg.at[slot, r, h],
            fg.at[1, r], y_right, y_left, f_out,
        )
        for r in range(2)
    ]

    LO, HI = pl.ds(0, 32), pl.ds(32, 32)
    part = (LO, HI)
    s_line = [
        Line(
            lambda h, s=s: sg.at[0, s, part[h]], lambda slot, h, s=s: sg.at[slot, s, part[h]],
            sg.at[1, s], z_right, z_left, s_out,
        )
        for s in range(NS)
    ]

    def prep_s(s, slots):
        for slot in slots:
            hi, lo = split(sg[slot, s])
            at = pl.ds(64 * slot, 64)
            s_hi[s, at, :] = hi
            s_lo[s, at, :] = lo

    def prep_d(u):
        for n, (slot, h) in enumerate(UNITS[u]):
            hi, lo = split(dg[slot, h])
            d_hi[u, :, lanes[n]] = hi
            d_lo[u, :, lanes[n]] = lo

    def prep_f(u, r):
        for n, (slot, h) in enumerate(UNITS[u]):
            for k in range(2):
                hi, lo = split(fg[slot, r, h, lanes[k], :].T)
                f_hi[u, r, lanes[n], lanes[k]] = hi
                f_lo[u, r, lanes[n], lanes[k]] = lo

    TOP, LOW = pl.ds(0, 16), pl.ds(16, 16)
    g = [dict() for _ in GROUPS]

    def at(n):
        s, first, count = GROUPS[n]
        return s, pl.ds(first, count), range(first, first + count)

    dx_out, ra_out, rb_out, f1_out, f0_out, g_right, g_left, h_out, q_out = sender(
        dx, ra, rb, flr.at[:, :, 0], flr.at[:, :, 1], flr.at[:, :, 0], flr.at[:, :, 0], flr.at[:, :, 0], dx
    )

    def p0(n):
        s, us, units = at(n)
        d = [jnp.concatenate([ref[u] for u in units], axis=1) for ref in (d_hi, d_lo)]
        tile = dot3(s_hi[s], s_lo[s], *d)
        for k, u in enumerate(units):
            mp[s, u] = tile[:, 256 * k : 256 * (k + 1)].reshape(2, 4, 32, 256)
        for name in ("dx", "ra", "rb", "f", "gr", "gl", "g2", "h", "q"):
            g[n][name] = recv()
        send(mp.at[s, us, oc], dx.at[s, us], partner, dx_out, g[n]["dx"])

    def p1(n):
        s, us, _ = at(n)
        wait(g[n]["dx"], dx.at[s, us])
        mp[s, us, c] += dx[s, us]
        send(mp.at[s, us, c, xo, TOP], ra.at[s, us], x_right, ra_out, g[n]["ra"])
        send(mp.at[s, us, c, xo, LOW], rb.at[s, us], x_left, rb_out, g[n]["rb"])
        send(mp.at[s, us, c, xr, LOW], flr.at[s, us, 0, LOW], x_right, f1_out, g[n]["f"])
        send(mp.at[s, us, c, xl, TOP], flr.at[s, us, 1, TOP], x_left, f1_out, g[n]["f"])

    def p2(n):
        s, us, _ = at(n)
        wait(g[n]["ra"], ra.at[s, us])
        mp[s, us, c, xr, TOP] += ra[s, us]
        send(mp.at[s, us, c, xr, TOP], flr.at[s, us, 0, TOP], x_right, f0_out, g[n]["f"])
        wait(g[n]["rb"], rb.at[s, us])
        mp[s, us, c, xl, LOW] += rb[s, us]
        send(mp.at[s, us, c, xl, LOW], flr.at[s, us, 1, LOW], x_left, f0_out, g[n]["f"])

    def p3(n):
        s, us, _ = at(n)
        wait(g[n]["f"], flr.at[s, us])
        mf[s, us, c, x] = mp[s, us, c, x] + flr[s, us, 0] + flr[s, us, 1]
        top, low, whole = mf.at[s, us, c, x, TOP], mf.at[s, us, c, x, LOW], mf.at[s, us, c, x]
        send(top, top, x_right, g_right, g[n]["gr"])
        send(low, low, x_left, g_left, g[n]["gl"])
        send(low, low, x_right, g_right, g[n]["g2"])
        send(top, top, x_left, g_left, g[n]["g2"])
        send(whole, whole, partner, q_out, g[n]["q"])

    def p4(n):
        s, us, _ = at(n)
        left, right = mf.at[s, us, c, xl], mf.at[s, us, c, xr]
        left_top, right_low = mf.at[s, us, c, xl, TOP], mf.at[s, us, c, xr, LOW]
        wait(g[n]["gr"], left_top)
        send(left_top, left_top, x_right, h_out, g[n]["h"])
        wait(g[n]["gl"], right_low)
        send(right_low, right_low, x_left, h_out, g[n]["h"])
        wait(g[n]["g2"], left)
        send(left, left, partner, q_out, g[n]["q"])
        send(right, right, partner, q_out, g[n]["q"])

    def p5(n):
        s, us, _ = at(n)
        wait(g[n]["h"], mf.at[s, us, c, xo])
        send(mf.at[s, us, c, xo], mf.at[s, us, c, xo], partner, q_out, g[n]["q"])

    begun = set()

    def p6(n, r):
        s, us, units = at(n)
        if "done" not in g[n]:
            wait(g[n]["q"], mf.at[s, us, oc])
            for u in units:
                m_hi[s, u], m_lo[s, u] = split(mf[s, u].reshape(256, 256))
            g[n]["done"] = True
        m = [jnp.concatenate([ref[s, u] for u in units], axis=1) for ref in (m_hi, m_lo)]
        f = [jnp.concatenate([ref[u, r] for u in units], axis=0) for ref in (f_hi, f_lo)]
        part = dot3(*m, *f).reshape(4, 64, 256)
        if (s, r) in begun:
            pacc[s, r] += part
        else:
            pacc[s, r] = part
            begun.add((s, r))

    w = {(s, r): [recv() for _ in range(3)] for s in range(NS) for r in range(2)}
    za_out, zb_out, z1_out, z0_out = sender(za, zb, zlr.at[:, :, 0], zlr.at[:, :, 0])

    def z1(s, r):
        a, b, f = w[s, r]
        send(pacc.at[s, r, 3, LO], za.at[s, r], z_right, za_out, a)
        send(pacc.at[s, r, 3, HI], zb.at[s, r], z_left, zb_out, b)
        send(pacc.at[s, r, 2, HI], zlr.at[s, r, 0, HI], z_right, z1_out, f)
        send(pacc.at[s, r, 1, LO], zlr.at[s, r, 1, LO], z_left, z1_out, f)

    def z2(s, r):
        a, b, f = w[s, r]
        wait(a, za.at[s, r])
        pacc[s, r, 2, LO] += za[s, r]
        send(pacc.at[s, r, 2, LO], zlr.at[s, r, 0, LO], z_right, z0_out, f)
        wait(b, zb.at[s, r])
        pacc[s, r, 1, HI] += zb[s, r]
        send(pacc.at[s, r, 1, HI], zlr.at[s, r, 1, HI], z_left, z0_out, f)

    parity = lax.rem(y, 2)
    t_core = lax.div(y, 2)
    diagonal = x == z

    def t_send_to(s, r, src, to_x, to_z, sem):
        return pltpu.make_async_remote_copy(
            src_ref=src, dst_ref=tb.at[parity, s], send_sem=sem, recv_sem=t_recv.at[s, parity],
            device_id=(to_x, t_core, to_z, 2 * c + r), device_id_type=MESH,
        )

    def t_direct(s, r):
        return t_send_to(s, r, pf.at[s, r], z, x, t_send.at[s, r])

    def t_first(s, r):
        slot, to = (z, dev(z=x)) if RELAY_AXIS == "z" else (x, dev(x=z))
        return pltpu.make_async_remote_copy(
            src_ref=pf.at[s, r], dst_ref=hop.at[s // 2, r, slot], send_sem=t_send.at[s, r],
            recv_sem=hop_recv.at[s // 2, r], device_id=to, device_id_type=MESH,
        )

    def t_second(s, r, d):
        slot = lax.rem(x + d, 4)
        to_x, to_z = (slot, x) if RELAY_AXIS == "z" else (x, slot)
        return t_send_to(s, r, hop.at[s // 2, r, slot], to_x, to_z, hop_send.at[0])

    def mirror(r):
        return jnp.logical_and(jnp.logical_and(diagonal, c == t_core), parity == r)

    def z3(s, r):
        wait(w[s, r][2], zlr.at[s, r])
        pf[s, r] = pacc[s, r, 0] + zlr[s, r, 0] + zlr[s, r, 1]

        @pl.when(mirror(r))
        def _():
            pltpu.make_async_copy(pf.at[s, r], tb.at[parity, s], t_recv.at[s, parity]).start()

        if s in RELAYED:

            @pl.when(jnp.logical_and(diagonal, jnp.logical_not(mirror(r))))
            def _():
                t_direct(s, r).start()

            @pl.when(jnp.logical_not(diagonal))
            def _():
                t_first(s, r).start()

        else:

            @pl.when(jnp.logical_not(mirror(r)))
            def _():
                t_direct(s, r).start()

    def relay(s, r):
        @pl.when(diagonal)
        def _():
            wait(hop_recv.at[s // 2, r], hop.at[0, 0, three])
            for d in range(1, 4):
                t_second(s, r, d).start()

    def t_wait(s, half):
        pltpu.make_async_copy(pf.at[s, 0], tb.at[half, s], t_recv.at[s, half]).wait()

    def history_gram():
        def step(n, acc):
            rows = pl.ds(pl.multiple_of(8 * n, 8), 8)
            acc = list(acc)
            for col in range(2):
                e = [eh[k, rows, lanes[col]] for k in range(6)]
                acc = [v + e[a] * e[b] for v, (a, b) in zip(acc, PAIRS)]
            return tuple(acc)

        acc = lax.fori_loop(0, 64, step, tuple(jnp.zeros((8, 128), F32) for _ in PAIRS))
        return [jnp.sum(v, axis=0, keepdims=True) for v in acc]

    plane, line = 4 * z + y, 2 * x + c
    sum_out = {n: sender(a.at[pl.ds(0, 15)], b.at[pl.ds(0, 7)]) for n, (a, b) in enumerate(((ha, hb), (na, nb)))}
    sum_in = {n: (recv(), recv()) for n in range(2)}

    def sum_plane(n, ref, rows):
        ref[plane] = jnp.concatenate(rows, axis=0)
        for d in range(1, 16):
            to = lax.rem(plane + d, 16)
            send(ref.at[plane], ref.at[plane], dev(z=lax.div(to, 4), y=lax.rem(to, 4)), sum_out[n][0], sum_in[n][0])

    def added(ref, count):
        total = ref[0]
        for k in range(1, count):
            total = total + ref[k]
        return total

    def sum_line(n, ref, before):
        wait(sum_in[n][0], before.at[pl.ds(0, 15)])
        ref[line] = added(before, 16)
        for d in range(1, 8):
            to = lax.rem(line + d, 8)
            send(ref.at[line], ref.at[line], dev(x=lax.div(to, 2), c=lax.rem(to, 2)), sum_out[n][1], sum_in[n][1])

    def sum_end(n, ref):
        wait(sum_in[n][1], ref.at[pl.ds(0, 7)])
        total = jnp.sum(added(ref, 8), axis=1, keepdims=True)
        return jnp.broadcast_to(total, (total.shape[0], 128))

    hist = []

    def first_gram():
        load_e.wait()
        hist.extend(history_gram() + [jnp.zeros((3, 128), F32)])

    def do_ps(s):
        s_line[s].second()
        s_line[s].third()
        prep_s(s, (0, 1, 2, 3))

    def do_pd(u):
        if u == 0:
            for copy in load_d:
                copy.wait()
        if u == 2:
            d_line.second()
        if u == 3:
            d_line.third()
        prep_d(u)

    def do_pf(u, r):
        if u == 0 and r == 0:
            for copy in load_f:
                copy.wait()
        if u == 2:
            f_line[r].second()
        if u == 3:
            f_line[r].third()
        prep_f(u, r)

    work = {
        "ys": lambda _: d_line.begin(), "yf": lambda _: d_line.forward(),
        "fs": lambda r: f_line[r].begin(), "ff": lambda r: f_line[r].forward(),
        "zs": lambda s: s_line[s].begin(), "zf": lambda s: s_line[s].forward(),
        "ps": do_ps, "pd": do_pd, "pf": do_pf, "hist": lambda _: first_gram(),
        "p0": p0, "p1": p1, "p2": p2, "p3": p3, "p4": p4, "p5": p5, "p6": p6,
        "z1": z1, "z2": z2, "z3": z3, "t": relay,
        "ha": lambda: sum_plane(0, ha, hist), "hb": lambda: sum_line(0, hb, ha), "hc": lambda: hist.append(sum_end(0, hb)),
    }
    for phase, *where in ORDER:
        work[phase](*where)

    for n in range(2):
        for r in range(2):
            own[halves[r], lanes[n]] = jnp.concatenate([pf[2 * n, r], pf[2 * n + 1, r]], axis=0).T
    load_h.wait()
    sums = [jnp.zeros((8, 128), F32) for _ in range(7)]
    for s in (1, 0, 2, 3):
        for half in range(2):
            t_wait(s, half)
            start = 256 * half + 64 * s

            def step(n, acc):
                rows = pl.ds(pl.multiple_of(start + 8 * n, 8), 8)
                for col in range(2):
                    e = own[rows, lanes[col]] - tb[half, s, pl.ds(pl.multiple_of(8 * n, 8), 8), lanes[col]]
                    err[rows, lanes[col]] = e
                    acc = tuple(acc[k] + eh[k, rows, lanes[col]] * e for k in range(6)) + (acc[6] + e * e,)
                return acc

            sums = lax.fori_loop(0, 8, step, tuple(sums))
    err_out = load(err, err_hbm)

    sum_plane(1, na, [jnp.sum(v, axis=0, keepdims=True) for v in sums] + [jnp.zeros((1, 128), F32)])
    sum_line(1, nb, na)
    new = sum_end(1, nb)

    gram = {}
    for n, (a, b) in enumerate(PAIRS):
        gram[b, a] = hist[-1][n : n + 1]
    for k in range(7):
        gram[6, k] = new[k : k + 1]
    low = {}
    for j in range(7):
        v = gram[j, j]
        for k in range(j):
            v = v - low[j, k] * low[j, k]
        low[j, j] = jnp.sqrt(v)
        for i in range(j + 1, 7):
            v = gram[i, j]
            for k in range(j):
                v = v - low[i, k] * low[j, k]
            low[i, j] = v / low[j, j]
    forward = []
    for i in range(7):
        v = jnp.ones((1, 128), F32)
        for k in range(i):
            v = v - low[i, k] * forward[k]
        forward.append(v / low[i, i])
    backward = [None] * 7
    for i in range(6, -1, -1):
        v = forward[i]
        for k in range(i + 1, 7):
            v = v - low[k, i] * backward[k]
        backward[i] = v / low[i, i]
    norm = backward[0]
    for v in backward[1:]:
        norm = norm + v
    weights = [v / norm for v in backward]
    lane = lax.broadcasted_iota(jnp.int32, (1, 128), 1)
    row = jnp.zeros((1, 128), F32)
    for k in range(7):
        row = jnp.where(lane == k, weights[k], row)
    w_ref[...] = row
    spread = [jnp.broadcast_to(v, (8, 128)) for v in weights]

    for r in range(2):

        def mix(n, carry):
            part = pl.ds(pl.multiple_of(8 * n, 8), 8)
            rows = pl.ds(pl.multiple_of(256 * r + 8 * n, 8), 8)
            for col in range(2):
                v = spread[6] * fg[0, r, col, part, :]
                for k in range(6):
                    v = v + spread[k] * fh[k, rows, lanes[col]]
                out[rows, lanes[col]] = v
            return carry

        lax.fori_loop(0, 32, mix, 0)
    next_out = load(out, next_hbm)
    for sem, ref in outgoing:
        wait(sem, ref)
    for s in range(NS):
        for r in range(2):

            @pl.when(jnp.logical_not(mirror(r)))
            def _():
                t_direct(s, r).wait_send()

    @pl.when(diagonal)
    def _():
        wait(hop_send.at[0], hop.at[:, :, three])

    err_out.wait()
    next_out.wait()


def body(fock_matrix, density, basis_gram, error_history, fock_history):
    any_ = pl.BlockSpec(memory_space=pl.ANY)
    v = lambda *shape: pltpu.VMEM(shape, F32)
    b = lambda *shape: pltpu.VMEM(shape, BF16)
    dma = pltpu.SemaphoreType.DMA
    block = jax.ShapeDtypeStruct((512, 256), F32)
    next_, err, w = pl.pallas_call(
        kernel,
        out_shape=(block, block, jax.ShapeDtypeStruct((1, 128), F32)),
        in_specs=[any_] * 5,
        out_specs=(any_, any_, pl.BlockSpec(memory_space=pltpu.VMEM)),
        scratch_shapes=[
            v(512, 256), v(4, NS, 64, 512), v(4, 2, 512, 128), v(4, 2, 2, 256, 128),
            b(NS, 256, 512), b(NS, 256, 512), b(NU, 512, 256), b(NU, 512, 256),
            b(NU, 2, 256, 256), b(NU, 2, 256, 256),
            v(NS, NU, 2, 4, 32, 256), v(NS, NU, 4, 32, 256),
            v(NS, NU, 16, 256), v(NS, NU, 16, 256), v(NS, NU, 2, 32, 256),
            v(NS, NU, 2, 4, 32, 256), b(NS, NU, 256, 256), b(NS, NU, 256, 256),
            v(NS, 2, 4, 64, 256), v(NS, 2, 32, 256), v(NS, 2, 32, 256), v(NS, 2, 2, 64, 256),
            v(NS, 2, 64, 256), v(2, NS, 64, 256), v(2, 2, 4, 64, 256),
            v(6, 512, 256), v(6, 512, 256), v(512, 256), v(512, 256), v(512, 256),
            v(16, 24, 128), v(8, 24, 128), v(16, 8, 128), v(8, 8, 128),
            dma((20,)), dma((N_RECV,)), dma((11,)),
            dma((NS, 2)), dma((NS, 2)), dma((2, 2)), dma((1,)),
        ],
        compiler_params=pltpu.CompilerParams(
            collective_id=0, has_side_effects=True, vmem_limit_bytes=60 * 1024 * 1024
        ),
    )(fock_matrix, density, basis_gram, error_history, fock_history)
    return next_, err, w[0, :7]


def solution(mesh):
    split_mesh = Mesh(mesh.devices.reshape(4, 2, 4, 4), ("x", "c", "z", "y"))
    two = P(("x", "c"), ("z", "y"))
    three = P(None, ("x", "c"), ("z", "y"))
    return jax.shard_map(
        body,
        mesh=split_mesh,
        in_specs=(two, two, two, three, three),
        out_specs=(two, two, P()),
        check_vma=False,
    )
```

time: 367 us -> 113 us (0.31)
  waiting for transfers between devices: 145 us -> 0 us
  Pallas kernels: 0 us -> 107 us
  blocking collectives: 65.2 us -> 0 us
  between operations: 50 us -> 0.64 us
  matrix products: 44.8 us -> 0 us
  local copies, waits for them, and re-layouts: 28.9 us -> 4.85 us
  starting transfers between devices: 21.5 us -> 0 us
  other arithmetic: 8.92 us -> 0 us
    pallas_call x0 -> x1, Pallas kernels: none -> 107 us  [body(): pl.pallas_call(kernel, out_shape=(block, block, jax.ShapeDtypeStruct((1,...]
    all_to_all x4 -> x0, blocking collectives: 65.2 us -> none  [from_everyone(): lax.all_to_all(jnp.broadcast_to(shard[None], (devices, *shard.shape)), ax...]
    all_gather x2 -> x0, waiting for transfers between devices: 62.8 us -> none  [the longest x1 38.2 us: body(): dens_rows = lax.all_gather(density, COL, axis=1, tiled=True)]
    ppermute x7 -> x0, waiting for transfers between devices: 54.4 us -> none  [from_partner(): return lax.ppermute(value, axis, pairs)]
    dot_general x4 -> x0, matrix products: 44.8 us -> none  [the longest x1 16.5 us: body(): jnp.dot(fock_rows, middle_cols, precision=highest, preferred_element_type...]
    all_to_all x2 -> x0, waiting for transfers between devices: 26.6 us -> none  [from_everyone(): lax.all_to_all(jnp.broadcast_to(shard[None], (devices, *shard.shape)), ax...]
    ppermute x7 -> x0, starting transfers between devices: 12.9 us -> none  [from_partner(): return lax.ppermute(value, axis, pairs)]
    unnamed x18 -> x2, local copies, waits for them, and re-layouts: 13.8 us -> 3.73 us
  transfers between devices with their start and end apart: 11 -> 0, of which waited for: 11 -> 0; matrix products, arithmetic and copies ran while one was open for 7% -> 0% of each run, Pallas kernels for 0% -> 0%
where the time goes in v2:
time: 113 us
  Pallas kernels  107 us (95%)
  local copies, waits for them, and re-layouts  4.85 us (4%)
    pallas_call x1, Pallas kernels, body(): pl.pallas_call(kernel, out_shape=(block, block, jax.ShapeDtypeStruct((1,...  107 us
    unnamed x2, local copies, waits for them, and re-layouts  3.73 us

profile of v2, /device:TPU:1, one launch (start us, length us, event | category | flops | bytes accessed | tf_op | source)
XLA Modules:
  0.0 112.9 jit_solution(5614443927740293846)
XLA Ops:
  0.6 107.4 %shard_map.76 = (f32[512,256]{1,0:T(8,128)}, f32[512,256]{1,0:T(8,128)}, f32[1,128]{1,0:T(1,128)}) custom-call(f32[512,256]{1,0:T(8,128)} %f_hbm.1, f32[512,256]{1,0:T(8,128)} %d_hbm.1, f32[512,256]{1,0:T(8,128)} %s_hbm.1, f32[6,512,256]{2,1,0:T(8,128)} %eh_hbm.1, f32[6,512,256]{2,1,0:T(8,128)} %fh_hbm.1), custom_call_target="tpu_custom_call" | custom-call | tf_op jit(solution)/shard_map/pallas_call | solution.py:545
  108.1 1.1 slice_bitcast_fusion
  109.2 1.9 %copy.10 = f32[512,256]{1,0:T(8,128)} copy(f32[512,256]{1,0:T(8,128)} %get-tuple-element.12) | data formatting | bytes 1048576
  111.1 1.9 %copy.11 = f32[512,256]{1,0:T(8,128)} copy(f32[512,256]{1,0:T(8,128)} %get-tuple-element.13) | data formatting | bytes 1048576

commit v3 on v2

--- a/solution.py
+++ b/solution.py
@@ -17,36 +17,35 @@
     (0, 1, 1),
     (1, 0, 2),
     (0, 2, 1),
-    (1, 2, 1),
+    (0, 3, 1),
+    (1, 2, 2),
     (2, 0, 2),
-    (0, 3, 1),
-    (1, 3, 1),
     (2, 2, 2),
     (3, 0, 2),
-    (3, 2, 2),
+    (3, 2, 1),
+    (3, 3, 1),
 )
 ORDER = (
-    ("ys", 0), ("zs", 0), ("pd", 0), ("hist", 0), ("zf", 0), ("zs", 1), ("ps", 0), ("p0", 0), ("zf", 1), ("zs", 2),
-    ("yf", 0), ("fs", 0), ("pd", 1), ("p0", 1), ("p1", 0), ("pf", 0, 0), ("pf", 0, 1), ("p1", 1), ("p2", 0),
-    ("ps", 1), ("p0", 2), ("p2", 1), ("zf", 2), ("zs", 3), ("pd", 2), ("p0", 3), ("p1", 2), ("p0", 4), ("p3", 0),
-    ("p1", 3), ("p3", 1), ("p1", 4), ("ps", 2), ("p0", 5), ("p2", 2), ("pd", 3), ("p0", 6), ("zf", 3), ("p0", 7),
-    ("p4", 0), ("p1", 5), ("p2", 3), ("p0", 8), ("p1", 6), ("p4", 1), ("p1", 7), ("p2", 4), ("p3", 2), ("ff", 0),
-    ("fs", 1), ("p1", 8), ("p5", 0), ("pf", 1, 0), ("ps", 3), ("p0", 9), ("p6", 0, 0), ("p6", 0, 1), ("p2", 5),
-    ("p2", 6), ("p0", 10), ("p5", 1), ("p1", 9), ("p2", 7), ("pf", 2, 0), ("p3", 3), ("p3", 4), ("p1", 10),
-    ("p6", 1, 0), ("pf", 3, 0), ("p4", 2), ("p2", 8), ("p3", 5), ("p3", 6), ("p2", 9), ("ff", 1), ("pf", 1, 1),
-    ("p6", 1, 1), ("p3", 7), ("p4", 3), ("p4", 4), ("p2", 10), ("pf", 2, 1), ("p5", 2), ("p3", 8), ("p6", 2, 0),
-    ("p6", 2, 1), ("p4", 5), ("pf", 3, 1), ("p4", 6), ("p3", 9), ("p4", 7), ("p5", 3), ("p5", 4), ("p3", 10),
-    ("p6", 3, 0), ("p6", 3, 1), ("p6", 4, 0), ("p6", 4, 1), ("p4", 8), ("p5", 5), ("p5", 6), ("p6", 5, 0),
-    ("p6", 5, 1), ("p4", 9), ("p5", 7), ("p6", 6, 0), ("p6", 6, 1), ("z1", 0, 0), ("z1", 0, 1), ("p4", 10),
-    ("p6", 7, 0), ("p6", 7, 1), ("p5", 8), ("z1", 1, 0), ("z1", 1, 1), ("p5", 9), ("p6", 8, 0), ("p6", 8, 1),
-    ("z2", 0, 0), ("p6", 9, 0), ("p5", 10), ("p6", 9, 1), ("z2", 0, 1), ("z1", 2, 0), ("z1", 2, 1), ("p6", 10, 0),
-    ("p6", 10, 1), ("z2", 1, 0), ("z1", 3, 0), ("z1", 3, 1), ("z2", 1, 1), ("z3", 0, 0), ("ha",), ("z3", 0, 1),
-    ("z2", 2, 0), ("z2", 2, 1), ("z3", 1, 0), ("z2", 3, 0), ("z2", 3, 1), ("z3", 1, 1), ("t", 0, 0), ("t", 0, 1),
-    ("z3", 2, 0), ("hb",), ("z3", 2, 1), ("z3", 3, 0), ("z3", 3, 1), ("hc",), ("t", 2, 0), ("t", 2, 1),
+    ("ys", 0), ("zs", 0), ("hist", 0), ("pd", 0), ("zf", 0), ("zs", 1), ("ps", 0), ("p0", 0), ("zf", 1), ("zs", 2),
+    ("yf", 0), ("fs", 0), ("pf", 0, 0), ("pf", 0, 1), ("p1", 0), ("pd", 1), ("p0", 1), ("p1", 1), ("p2", 0),
+    ("ps", 1), ("p0", 2), ("zf", 2), ("zs", 3), ("p2", 1), ("pd", 2), ("p0", 3), ("p3", 0), ("p1", 2), ("p1", 3),
+    ("p3", 1), ("ps", 2), ("p0", 6), ("p4", 0), ("zf", 3), ("pd", 3), ("p2", 2), ("p0", 4), ("p1", 6), ("p2", 3),
+    ("p0", 5), ("p0", 7), ("p5", 0), ("p1", 4), ("p4", 1), ("p1", 5), ("ps", 3), ("ff", 0), ("fs", 1), ("p6", 0, 0),
+    ("p2", 6), ("p6", 0, 1), ("pf", 1, 0), ("p0", 8), ("p1", 7), ("p2", 4), ("p0", 9), ("p5", 1), ("pf", 2, 0),
+    ("p2", 5), ("p0", 10), ("p3", 2), ("p6", 1, 0), ("p2", 7), ("pf", 3, 0), ("p3", 3), ("p3", 4), ("p3", 5),
+    ("p4", 2), ("ff", 1), ("pf", 1, 1), ("p6", 1, 1), ("p1", 8), ("p4", 3), ("p4", 4), ("p3", 6), ("p4", 5),
+    ("pf", 2, 1), ("p5", 2), ("p2", 8), ("p6", 2, 0), ("p6", 2, 1), ("p5", 3), ("p5", 4), ("p1", 9), ("pf", 3, 1),
+    ("p1", 10), ("p3", 7), ("p6", 3, 0), ("p4", 6), ("p6", 3, 1), ("p5", 5), ("p6", 4, 0), ("z1", 0, 0), ("p6", 4, 1),
+    ("z1", 0, 1), ("p2", 9), ("p6", 5, 0), ("z1", 1, 0), ("p2", 10), ("p6", 5, 1), ("p3", 8), ("z1", 1, 1), ("p4", 7),
+    ("z2", 0, 0), ("p5", 6), ("p3", 9), ("p3", 10), ("z2", 0, 1), ("p6", 6, 0), ("p6", 6, 1), ("p4", 8), ("z2", 1, 0),
+    ("p5", 7), ("p4", 9), ("z2", 1, 1), ("p6", 7, 0), ("z1", 2, 0), ("p4", 10), ("p6", 7, 1), ("z1", 2, 1), ("p5", 8),
+    ("z3", 0, 0), ("ha",), ("p5", 9), ("z3", 0, 1), ("z3", 1, 0), ("p6", 8, 0), ("z3", 1, 1), ("p5", 10),
+    ("p6", 8, 1), ("z2", 2, 0), ("p6", 9, 0), ("p6", 9, 1), ("p6", 10, 0), ("z1", 3, 0), ("p6", 10, 1), ("z1", 3, 1),
+    ("z2", 2, 1), ("z3", 2, 0), ("u", 1), ("z2", 3, 0), ("t", 0, 0), ("t", 0, 1), ("z2", 3, 1), ("z3", 2, 1),
+    ("z3", 3, 0), ("z3", 3, 1), ("hb",), ("own",), ("u", 3), ("t", 2, 0), ("t", 2, 1),
 )
 N_RECV = 49 + 9 * len(GROUPS)
 RELAYED = (0, 2)
-RELAY_AXIS = "z"
 
 
 def split(v):
@@ -61,18 +60,18 @@
 
 
 def kernel(
-    f_hbm, d_hbm, s_hbm, eh_hbm, fh_hbm, next_hbm, err_hbm, w_ref,
+    f_hbm, d_hbm, s_hbm, eh_hbm, fh_hbm, out, err, w_ref,
     s_in, sg, dg, fg, s_hi, s_lo, d_hi, d_lo, f_hi, f_lo,
-    mp, dx, ra, rb, flr, mf, m_hi, m_lo, pacc, za, zb, zlr, pf, tb, hop,
-    eh, fh, own, err, out, ha, hb, na, nb,
-    send_sem, recv_sem, local_sem, t_send, t_recv, hop_recv, hop_send,
+    mp, dx, ra, rb, flr, mf, m_hi, m_lo, pacc, za, zb, zlr, pf, tb, hop, turn,
+    eh, fh, own, ha, hb, na, nb,
+    send_sem, recv_sem, local_sem, t_send, t_recv, hop_recv, hop_send, turn_recv, turn_send,
 ):
     x, c, z, y = (lax.axis_index(n) for n in ("x", "c", "z", "y"))
     xr, xl, xo = lax.rem(x + 1, 4), lax.rem(x + 3, 4), lax.rem(x + 2, 4)
     dev = lambda x=x, c=c, z=z, y=y: (x, c, z, y)
     x_right, x_left = dev(x=xr), dev(x=xl)
-    y_right, y_left = dev(y=lax.rem(y + 1, 4)), dev(y=lax.rem(y + 3, 4))
-    z_right, z_left = dev(z=lax.rem(z + 1, 4)), dev(z=lax.rem(z + 3, 4))
+    d_right, d_left = dev(z=lax.rem(z + 1, 4)), dev(z=lax.rem(z + 3, 4))
+    s_right, s_left = dev(y=lax.rem(y + 1, 4)), dev(y=lax.rem(y + 3, 4))
     oc = 1 - c
     partner = dev(c=oc)
 
@@ -110,7 +109,7 @@
     halves = [pl.ds(0, 256), pl.ds(256, 256)]
 
     barrier = pltpu.get_barrier_semaphore()
-    for to in (x_right, x_left, y_right, y_left, z_right, z_left, partner):
+    for to in (x_right, x_left, d_right, d_left, s_right, s_left, partner):
         pl.semaphore_signal(barrier, inc=1, device_id=to, device_id_type=MESH)
     load_s = load(s_hbm, s_in)
     load_d = [load(d_hbm.at[:, lanes[h]], dg.at[0, h]) for h in range(2)]
@@ -153,11 +152,11 @@
         def third(self):
             wait(self.sems[2], self.size)
 
-    d_line = Line(lambda h: d_hbm.at[:, lanes[h]], lambda slot, h: dg.at[slot, h], dg.at[1], y_right, y_left, d_out)
+    d_line = Line(lambda h: d_hbm.at[:, lanes[h]], lambda slot, h: dg.at[slot, h], dg.at[1], d_right, d_left, d_out)
     f_line = [
         Line(
             lambda h, r=r: f_hbm.at[halves[r], lanes[h]], lambda slot, h, r=r: fg.at[slot, r, h],
-            fg.at[1, r], y_right, y_left, f_out,
+            fg.at[1, r], d_right, d_left, f_out,
         )
         for r in range(2)
     ]
@@ -167,7 +166,7 @@
     s_line = [
         Line(
             lambda h, s=s: sg.at[0, s, part[h]], lambda slot, h, s=s: sg.at[slot, s, part[h]],
-            sg.at[1, s], z_right, z_left, s_out,
+            sg.at[1, s], s_right, s_left, s_out,
         )
         for s in range(NS)
     ]
@@ -282,81 +281,89 @@
 
     def z1(s, r):
         a, b, f = w[s, r]
-        send(pacc.at[s, r, 3, LO], za.at[s, r], z_right, za_out, a)
-        send(pacc.at[s, r, 3, HI], zb.at[s, r], z_left, zb_out, b)
-        send(pacc.at[s, r, 2, HI], zlr.at[s, r, 0, HI], z_right, z1_out, f)
-        send(pacc.at[s, r, 1, LO], zlr.at[s, r, 1, LO], z_left, z1_out, f)
+        send(pacc.at[s, r, 3, LO], za.at[s, r], s_right, za_out, a)
+        send(pacc.at[s, r, 3, HI], zb.at[s, r], s_left, zb_out, b)
+        send(pacc.at[s, r, 2, HI], zlr.at[s, r, 0, HI], s_right, z1_out, f)
+        send(pacc.at[s, r, 1, LO], zlr.at[s, r, 1, LO], s_left, z1_out, f)
 
     def z2(s, r):
         a, b, f = w[s, r]
         wait(a, za.at[s, r])
         pacc[s, r, 2, LO] += za[s, r]
-        send(pacc.at[s, r, 2, LO], zlr.at[s, r, 0, LO], z_right, z0_out, f)
+        send(pacc.at[s, r, 2, LO], zlr.at[s, r, 0, LO], s_right, z0_out, f)
         wait(b, zb.at[s, r])
         pacc[s, r, 1, HI] += zb[s, r]
-        send(pacc.at[s, r, 1, HI], zlr.at[s, r, 1, HI], z_left, z0_out, f)
+        send(pacc.at[s, r, 1, HI], zlr.at[s, r, 1, HI], s_left, z0_out, f)
 
     parity = lax.rem(y, 2)
     t_core = lax.div(y, 2)
     diagonal = x == z
+    stays = [jnp.logical_and(c == t_core, parity == r) for r in range(2)]
 
     def t_send_to(s, r, src, to_x, to_z, sem):
         return pltpu.make_async_remote_copy(
-            src_ref=src, dst_ref=tb.at[parity, s], send_sem=sem, recv_sem=t_recv.at[s, parity],
+            src_ref=src, dst_ref=tb.at[s, parity], send_sem=sem, recv_sem=t_recv.at[s],
             device_id=(to_x, t_core, to_z, 2 * c + r), device_id_type=MESH,
         )
 
-    def t_direct(s, r):
-        return t_send_to(s, r, pf.at[s, r], z, x, t_send.at[s, r])
-
     def t_first(s, r):
-        slot, to = (z, dev(z=x)) if RELAY_AXIS == "z" else (x, dev(x=z))
+        src = pf.at[s, r]
+        yield diagonal, stays[r], tb.at[s, parity], t_recv.at[s], (x, t_core, z, 2 * c + r)
+        if s in RELAYED:
+            k = RELAYED.index(s)
+            yield jnp.logical_not(diagonal), None, hop.at[k, r, z], hop_recv.at[k, r], dev(z=x)
+        else:
+            k = s // 2
+            yield jnp.logical_not(diagonal), stays[r], turn.at[k, parity], turn_recv.at[k], (x, t_core, z, 2 * c + r)
+
+    def t_copy(s, r, dst, sem, to):
         return pltpu.make_async_remote_copy(
-            src_ref=pf.at[s, r], dst_ref=hop.at[s // 2, r, slot], send_sem=t_send.at[s, r],
-            recv_sem=hop_recv.at[s // 2, r], device_id=to, device_id_type=MESH,
+            src_ref=pf.at[s, r], dst_ref=dst, send_sem=t_send.at[s, r], recv_sem=sem, device_id=to, device_id_type=MESH,
         )
 
     def t_second(s, r, d):
         slot = lax.rem(x + d, 4)
-        to_x, to_z = (slot, x) if RELAY_AXIS == "z" else (x, slot)
-        return t_send_to(s, r, hop.at[s // 2, r, slot], to_x, to_z, hop_send.at[0])
-
-    def mirror(r):
-        return jnp.logical_and(jnp.logical_and(diagonal, c == t_core), parity == r)
+        return t_send_to(s, r, hop.at[RELAYED.index(s), r, slot], slot, x, hop_send.at[0])
+
+    def turned(s):
+        return pltpu.make_async_remote_copy(
+            src_ref=turn.at[s // 2], dst_ref=tb.at[s], send_sem=turn_send.at[0], recv_sem=t_recv.at[s],
+            device_id=dev(x=z, z=x), device_id_type=MESH,
+        )
 
     def z3(s, r):
         wait(w[s, r][2], zlr.at[s, r])
         pf[s, r] = pacc[s, r, 0] + zlr[s, r, 0] + zlr[s, r, 1]
-
-        @pl.when(mirror(r))
+        for case, local_case, dst, sem, to in t_first(s, r):
+            away = case if local_case is None else jnp.logical_and(case, jnp.logical_not(local_case))
+
+            @pl.when(away)
+            def _(dst=dst, sem=sem, to=to):
+                t_copy(s, r, dst, sem, to).start()
+
+            if local_case is not None:
+
+                @pl.when(jnp.logical_and(case, local_case))
+                def _(dst=dst, sem=sem):
+                    pltpu.make_async_copy(pf.at[s, r], dst, sem).start()
+
+    def pass_on(s):
+        @pl.when(jnp.logical_not(diagonal))
         def _():
-            pltpu.make_async_copy(pf.at[s, r], tb.at[parity, s], t_recv.at[s, parity]).start()
-
-        if s in RELAYED:
-
-            @pl.when(jnp.logical_and(diagonal, jnp.logical_not(mirror(r))))
-            def _():
-                t_direct(s, r).start()
-
-            @pl.when(jnp.logical_not(diagonal))
-            def _():
-                t_first(s, r).start()
-
-        else:
-
-            @pl.when(jnp.logical_not(mirror(r)))
-            def _():
-                t_direct(s, r).start()
+            wait(turn_recv.at[s // 2], turn.at[s // 2])
+            turned(s).start()
 
     def relay(s, r):
         @pl.when(diagonal)
         def _():
-            wait(hop_recv.at[s // 2, r], hop.at[0, 0, three])
+            wait(hop_recv.at[RELAYED.index(s), r], hop.at[0, 0, three])
             for d in range(1, 4):
                 t_second(s, r, d).start()
 
-    def t_wait(s, half):
-        pltpu.make_async_copy(pf.at[s, 0], tb.at[half, s], t_recv.at[s, half]).wait()
+    def turn_own():
+        for n in range(2):
+            for r in range(2):
+                own[halves[r], lanes[n]] = jnp.concatenate([pf[2 * n, r], pf[2 * n + 1, r]], axis=0).T
 
     def history_gram():
         def step(n, acc):
@@ -435,35 +442,32 @@
         "zs": lambda s: s_line[s].begin(), "zf": lambda s: s_line[s].forward(),
         "ps": do_ps, "pd": do_pd, "pf": do_pf, "hist": lambda _: first_gram(),
         "p0": p0, "p1": p1, "p2": p2, "p3": p3, "p4": p4, "p5": p5, "p6": p6,
-        "z1": z1, "z2": z2, "z3": z3, "t": relay,
-        "ha": lambda: sum_plane(0, ha, hist), "hb": lambda: sum_line(0, hb, ha), "hc": lambda: hist.append(sum_end(0, hb)),
+        "z1": z1, "z2": z2, "z3": z3, "t": relay, "u": pass_on, "own": turn_own,
+        "ha": lambda: sum_plane(0, ha, hist), "hb": lambda: sum_line(0, hb, ha),
     }
     for phase, *where in ORDER:
         work[phase](*where)
 
-    for n in range(2):
-        for r in range(2):
-            own[halves[r], lanes[n]] = jnp.concatenate([pf[2 * n, r], pf[2 * n + 1, r]], axis=0).T
     load_h.wait()
     sums = [jnp.zeros((8, 128), F32) for _ in range(7)]
-    for s in (1, 0, 2, 3):
+    for s in (1, 0, 3, 2):
+        wait(t_recv.at[s], tb.at[s])
         for half in range(2):
-            t_wait(s, half)
             start = 256 * half + 64 * s
 
             def step(n, acc):
                 rows = pl.ds(pl.multiple_of(start + 8 * n, 8), 8)
                 for col in range(2):
-                    e = own[rows, lanes[col]] - tb[half, s, pl.ds(pl.multiple_of(8 * n, 8), 8), lanes[col]]
+                    e = own[rows, lanes[col]] - tb[s, half, pl.ds(pl.multiple_of(8 * n, 8), 8), lanes[col]]
                     err[rows, lanes[col]] = e
                     acc = tuple(acc[k] + eh[k, rows, lanes[col]] * e for k in range(6)) + (acc[6] + e * e,)
                 return acc
 
             sums = lax.fori_loop(0, 8, step, tuple(sums))
-    err_out = load(err, err_hbm)
 
     sum_plane(1, na, [jnp.sum(v, axis=0, keepdims=True) for v in sums] + [jnp.zeros((1, 128), F32)])
     sum_line(1, nb, na)
+    hist.append(sum_end(0, hb))
     new = sum_end(1, nb)
 
     gram = {}
@@ -518,22 +522,23 @@
             return carry
 
         lax.fori_loop(0, 32, mix, 0)
-    next_out = load(out, next_hbm)
     for sem, ref in outgoing:
         wait(sem, ref)
     for s in range(NS):
         for r in range(2):
-
-            @pl.when(jnp.logical_not(mirror(r)))
+            here = jnp.logical_and(diagonal, stays[r]) if s in RELAYED else stays[r]
+
+            @pl.when(jnp.logical_not(here))
             def _():
-                t_direct(s, r).wait_send()
+                wait(t_send.at[s, r], pf.at[s, r])
+
+    @pl.when(jnp.logical_not(diagonal))
+    def _():
+        wait(turn_send.at[0], turn)
 
     @pl.when(diagonal)
     def _():
         wait(hop_send.at[0], hop.at[:, :, three])
-
-    err_out.wait()
-    next_out.wait()
 
 
 def body(fock_matrix, density, basis_gram, error_history, fock_history):
@@ -541,12 +546,12 @@
     v = lambda *shape: pltpu.VMEM(shape, F32)
     b = lambda *shape: pltpu.VMEM(shape, BF16)
     dma = pltpu.SemaphoreType.DMA
-    block = jax.ShapeDtypeStruct((512, 256), F32)
+    block = pltpu.VMEM((512, 256), F32)
     next_, err, w = pl.pallas_call(
         kernel,
-        out_shape=(block, block, jax.ShapeDtypeStruct((1, 128), F32)),
+        out_shape=(block, block, pltpu.VMEM((1, 128), F32)),
         in_specs=[any_] * 5,
-        out_specs=(any_, any_, pl.BlockSpec(memory_space=pltpu.VMEM)),
+        out_specs=(pl.BlockSpec(memory_space=pltpu.VMEM),) * 3,
         scratch_shapes=[
             v(512, 256), v(4, NS, 64, 512), v(4, 2, 512, 128), v(4, 2, 2, 256, 128),
             b(NS, 256, 512), b(NS, 256, 512), b(NU, 512, 256), b(NU, 512, 256),
@@ -555,11 +560,11 @@
             v(NS, NU, 16, 256), v(NS, NU, 16, 256), v(NS, NU, 2, 32, 256),
             v(NS, NU, 2, 4, 32, 256), b(NS, NU, 256, 256), b(NS, NU, 256, 256),
             v(NS, 2, 4, 64, 256), v(NS, 2, 32, 256), v(NS, 2, 32, 256), v(NS, 2, 2, 64, 256),
-            v(NS, 2, 64, 256), v(2, NS, 64, 256), v(2, 2, 4, 64, 256),
-            v(6, 512, 256), v(6, 512, 256), v(512, 256), v(512, 256), v(512, 256),
+            v(NS, 2, 64, 256), v(NS, 2, 64, 256), v(2, 2, 4, 64, 256), v(2, 2, 64, 256),
+            v(6, 512, 256), v(6, 512, 256), v(512, 256),
             v(16, 24, 128), v(8, 24, 128), v(16, 8, 128), v(8, 8, 128),
-            dma((20,)), dma((N_RECV,)), dma((11,)),
-            dma((NS, 2)), dma((NS, 2)), dma((2, 2)), dma((1,)),
+            dma((20,)), dma((N_RECV,)), dma((9,)),
+            dma((NS, 2)), dma((NS,)), dma((2, 2)), dma((1,)), dma((2,)), dma((1,)),
         ],
         compiler_params=pltpu.CompilerParams(
             collective_id=0, has_side_effects=True, vmem_limit_bytes=60 * 1024 * 1024

time: 113 us -> 98.4 us (0.87)
  Pallas kernels: 107 us -> 95.6 us
  local copies, waits for them, and re-layouts: 4.85 us -> 2.1 us
    pallas_call x1, Pallas kernels: 107 us -> 95.6 us  [body(): pl.pallas_call(kernel, out_shape=(block, block, pltpu.VMEM((1, 128), F32)...]
    unnamed x2, local copies, waits for them, and re-layouts: 3.73 us -> 1.59 us
where the time goes in v3:
time: 98.4 us; the launch traced here: 98.3 us
  Pallas kernels  95.6 us (97%)
  local copies, waits for them, and re-layouts  2.1 us (2%)
    pallas_call x1, Pallas kernels, body(): pl.pallas_call(kernel, out_shape=(block, block, pltpu.VMEM((1, 128), F32)...  95.6 us

profile of v3, /device:TPU:1, one launch (start us, length us, event | category | flops | bytes accessed | tf_op | source)
XLA Modules:
  0.0 98.3 jit_solution(1018825291627943428)
XLA Ops:
  0.6 95.6 %shard_map.76 = (f32[512,256]{1,0:T(8,128)S(1)}, f32[512,256]{1,0:T(8,128)S(1)}, f32[1,128]{1,0:T(1,128)S(1)}) custom-call(f32[512,256]{1,0:T(8,128)} %f_hbm.1, f32[512,256]{1,0:T(8,128)} %d_hbm.1, f32[512,256]{1,0:T(8,128)} %s_hbm.1, f32[6,512,256]{2,1,0:T(8,128)} %eh_hbm.1, f32[6,512,256]{2,1,0:T(8,128)} %fh_hbm.1), custom_call_target="tpu_custom_call" | custom-call | tf_op jit(solution)/shard_map/pallas_call | solution.py:550
  96.2 0.8 copy.10
  97.0 0.5 slice_bitcast_fusion
  97.5 0.8 copy.11

commit v4 on v3

--- a/solution.py
+++ b/solution.py
@@ -13,39 +13,31 @@
 NS, NU = 4, 4
 PAIRS = [(a, b) for a in range(6) for b in range(a, 6)]
 GROUPS = (
-    (0, 0, 1),
-    (0, 1, 1),
-    (1, 0, 2),
-    (0, 2, 1),
-    (0, 3, 1),
-    (1, 2, 2),
-    (2, 0, 2),
-    (2, 2, 2),
-    (3, 0, 2),
-    (3, 2, 1),
+    (0, 0, 1), (0, 1, 1), (1, 0, 2), (0, 2, 1), (0, 3, 1), (1, 2, 2), (2, 0, 2), (2, 2, 2), (3, 0, 2), (3, 2, 1),
     (3, 3, 1),
 )
 ORDER = (
-    ("ys", 0), ("zs", 0), ("hist", 0), ("pd", 0), ("zf", 0), ("zs", 1), ("ps", 0), ("p0", 0), ("zf", 1), ("zs", 2),
-    ("yf", 0), ("fs", 0), ("pf", 0, 0), ("pf", 0, 1), ("p1", 0), ("pd", 1), ("p0", 1), ("p1", 1), ("p2", 0),
-    ("ps", 1), ("p0", 2), ("zf", 2), ("zs", 3), ("p2", 1), ("pd", 2), ("p0", 3), ("p3", 0), ("p1", 2), ("p1", 3),
-    ("p3", 1), ("ps", 2), ("p0", 6), ("p4", 0), ("zf", 3), ("pd", 3), ("p2", 2), ("p0", 4), ("p1", 6), ("p2", 3),
-    ("p0", 5), ("p0", 7), ("p5", 0), ("p1", 4), ("p4", 1), ("p1", 5), ("ps", 3), ("ff", 0), ("fs", 1), ("p6", 0, 0),
-    ("p2", 6), ("p6", 0, 1), ("pf", 1, 0), ("p0", 8), ("p1", 7), ("p2", 4), ("p0", 9), ("p5", 1), ("pf", 2, 0),
-    ("p2", 5), ("p0", 10), ("p3", 2), ("p6", 1, 0), ("p2", 7), ("pf", 3, 0), ("p3", 3), ("p3", 4), ("p3", 5),
-    ("p4", 2), ("ff", 1), ("pf", 1, 1), ("p6", 1, 1), ("p1", 8), ("p4", 3), ("p4", 4), ("p3", 6), ("p4", 5),
-    ("pf", 2, 1), ("p5", 2), ("p2", 8), ("p6", 2, 0), ("p6", 2, 1), ("p5", 3), ("p5", 4), ("p1", 9), ("pf", 3, 1),
-    ("p1", 10), ("p3", 7), ("p6", 3, 0), ("p4", 6), ("p6", 3, 1), ("p5", 5), ("p6", 4, 0), ("z1", 0, 0), ("p6", 4, 1),
-    ("z1", 0, 1), ("p2", 9), ("p6", 5, 0), ("z1", 1, 0), ("p2", 10), ("p6", 5, 1), ("p3", 8), ("z1", 1, 1), ("p4", 7),
-    ("z2", 0, 0), ("p5", 6), ("p3", 9), ("p3", 10), ("z2", 0, 1), ("p6", 6, 0), ("p6", 6, 1), ("p4", 8), ("z2", 1, 0),
-    ("p5", 7), ("p4", 9), ("z2", 1, 1), ("p6", 7, 0), ("z1", 2, 0), ("p4", 10), ("p6", 7, 1), ("z1", 2, 1), ("p5", 8),
-    ("z3", 0, 0), ("ha",), ("p5", 9), ("z3", 0, 1), ("z3", 1, 0), ("p6", 8, 0), ("z3", 1, 1), ("p5", 10),
-    ("p6", 8, 1), ("z2", 2, 0), ("p6", 9, 0), ("p6", 9, 1), ("p6", 10, 0), ("z1", 3, 0), ("p6", 10, 1), ("z1", 3, 1),
-    ("z2", 2, 1), ("z3", 2, 0), ("u", 1), ("z2", 3, 0), ("t", 0, 0), ("t", 0, 1), ("z2", 3, 1), ("z3", 2, 1),
-    ("z3", 3, 0), ("z3", 3, 1), ("hb",), ("own",), ("u", 3), ("t", 2, 0), ("t", 2, 1),
+    ("ys", 0), ("zs", 0), ("zs", 1), ("zf", 0), ("zf", 1), ("zs", 3), ("yf", 0), ("pd", 0), ("zs", 2), ("fs", 0),
+    ("pd", 1), ("ps", 0), ("p0", 1), ("p0", 0), ("ps", 1), ("p0", 2), ("p1", 1), ("p1", 0), ("p1", 2), ("hist", 0),
+    ("zf", 3), ("p2", 1), ("pd", 2), ("p2", 0), ("p0", 3), ("zf", 2), ("p2", 2), ("p1", 3), ("p3", 1), ("p3", 0),
+    ("p3", 2), ("pd", 3), ("p0", 4), ("p0", 5), ("p2", 3), ("p4", 1), ("p1", 4), ("ps", 2), ("p4", 0), ("ps", 3),
+    ("pf", 0, 0), ("p1", 5), ("p0", 7), ("ff", 0), ("p3", 3), ("p2", 4), ("p1", 7), ("p0", 6), ("fs", 1), ("p2", 5),
+    ("p4", 2), ("p4", 3), ("p3", 4), ("p0", 10), ("p5", 0), ("p1", 6), ("p0", 9), ("p5", 1), ("pf", 1, 0), ("p3", 5),
+    ("p6", 1, 0), ("p0", 8), ("p4", 4), ("p1", 9), ("p2", 7), ("p5", 3), ("ff", 1), ("pf", 0, 1), ("pf", 1, 1),
+    ("pf", 3, 0), ("p6", 0, 0), ("p1", 10), ("p2", 6), ("pf", 2, 0), ("p4", 5), ("p5", 2), ("p1", 8), ("p5", 4),
+    ("p6", 3, 0), ("p6", 4, 0), ("z1", 0, 0), ("p6", 0, 1), ("pf", 2, 1), ("p3", 7), ("p6", 1, 1), ("p2", 9),
+    ("p6", 3, 1), ("pf", 3, 1), ("p6", 4, 1), ("z1", 0, 1), ("p3", 6), ("p5", 5), ("p2", 10), ("p6", 2, 0),
+    ("p6", 2, 1), ("z2", 0, 0), ("p6", 5, 0), ("z1", 1, 0), ("p2", 8), ("p4", 7), ("p3", 9), ("z2", 0, 1),
+    ("p6", 5, 1), ("z1", 1, 1), ("p4", 6), ("p3", 10), ("z2", 1, 0), ("p3", 8), ("z3", 0, 0), ("p5", 7), ("z3", 0, 1),
+    ("ha",), ("p4", 9), ("z2", 1, 1), ("p5", 6), ("p6", 7, 0), ("p6", 7, 1), ("p4", 10), ("z3", 1, 0), ("p6", 6, 0),
+    ("p6", 6, 1), ("p4", 8), ("z1", 2, 1), ("p5", 9), ("z3", 1, 1), ("z1", 2, 0), ("p5", 10), ("p6", 9, 0), ("p5", 8),
+    ("p6", 10, 0), ("z2", 2, 1), ("p6", 10, 1), ("p6", 8, 0), ("z1", 3, 0), ("p6", 9, 1), ("u", 1), ("z2", 2, 0),
+    ("p6", 8, 1), ("z1", 3, 1), ("t", 1, 1), ("u", 0), ("z2", 3, 0), ("z3", 2, 1), ("t", 0, 1), ("z2", 3, 1),
+    ("t", 1, 0), ("z3", 2, 0), ("z3", 3, 0), ("t", 0, 0), ("z3", 3, 1), ("own",), ("t", 2, 1), ("t", 2, 0), ("u", 2),
+    ("t", 3, 0), ("t", 3, 1), ("hb",),
 )
-N_RECV = 49 + 9 * len(GROUPS)
-RELAYED = (0, 2)
+N_RECV = 41 + 7 * len(GROUPS)
+TURNED = 3
 
 
 def split(v):
@@ -62,7 +54,7 @@
 def kernel(
     f_hbm, d_hbm, s_hbm, eh_hbm, fh_hbm, out, err, w_ref,
     s_in, sg, dg, fg, s_hi, s_lo, d_hi, d_lo, f_hi, f_lo,
-    mp, dx, ra, rb, flr, mf, m_hi, m_lo, pacc, za, zb, zlr, pf, tb, hop, turn,
+    mp, dx, rab, flr, mf, m_hi, m_lo, pacc, zab, zlr, pf, tb, hop, turn,
     eh, fh, own, ha, hb, na, nb,
     send_sem, recv_sem, local_sem, t_send, t_recv, hop_recv, hop_send, turn_recv, turn_send,
 ):
@@ -198,8 +190,8 @@
         s, first, count = GROUPS[n]
         return s, pl.ds(first, count), range(first, first + count)
 
-    dx_out, ra_out, rb_out, f1_out, f0_out, g_right, g_left, h_out, q_out = sender(
-        dx, ra, rb, flr.at[:, :, 0], flr.at[:, :, 1], flr.at[:, :, 0], flr.at[:, :, 0], flr.at[:, :, 0], dx
+    dx_out, r_out, f1_out, f0_out, g_right, g_left, h_out, q_out = sender(
+        dx, rab, flr.at[:, :, 0], flr.at[:, :, 1], flr.at[:, :, 0], flr.at[:, :, 0], flr.at[:, :, 0], dx
     )
 
     def p0(n):
@@ -208,7 +200,7 @@
         tile = dot3(s_hi[s], s_lo[s], *d)
         for k, u in enumerate(units):
             mp[s, u] = tile[:, 256 * k : 256 * (k + 1)].reshape(2, 4, 32, 256)
-        for name in ("dx", "ra", "rb", "f", "gr", "gl", "g2", "h", "q"):
+        for name in ("dx", "r", "f", "g1", "g2", "h", "q"):
             g[n][name] = recv()
         send(mp.at[s, us, oc], dx.at[s, us], partner, dx_out, g[n]["dx"])
 
@@ -216,18 +208,17 @@
         s, us, _ = at(n)
         wait(g[n]["dx"], dx.at[s, us])
         mp[s, us, c] += dx[s, us]
-        send(mp.at[s, us, c, xo, TOP], ra.at[s, us], x_right, ra_out, g[n]["ra"])
-        send(mp.at[s, us, c, xo, LOW], rb.at[s, us], x_left, rb_out, g[n]["rb"])
+        send(mp.at[s, us, c, xo, TOP], rab.at[s, us, 0], x_right, r_out, g[n]["r"])
+        send(mp.at[s, us, c, xo, LOW], rab.at[s, us, 1], x_left, r_out, g[n]["r"])
         send(mp.at[s, us, c, xr, LOW], flr.at[s, us, 0, LOW], x_right, f1_out, g[n]["f"])
         send(mp.at[s, us, c, xl, TOP], flr.at[s, us, 1, TOP], x_left, f1_out, g[n]["f"])
 
     def p2(n):
         s, us, _ = at(n)
-        wait(g[n]["ra"], ra.at[s, us])
-        mp[s, us, c, xr, TOP] += ra[s, us]
+        wait(g[n]["r"], rab.at[s, us])
+        mp[s, us, c, xr, TOP] += rab[s, us, 0]
         send(mp.at[s, us, c, xr, TOP], flr.at[s, us, 0, TOP], x_right, f0_out, g[n]["f"])
-        wait(g[n]["rb"], rb.at[s, us])
-        mp[s, us, c, xl, LOW] += rb[s, us]
+        mp[s, us, c, xl, LOW] += rab[s, us, 1]
         send(mp.at[s, us, c, xl, LOW], flr.at[s, us, 1, LOW], x_left, f0_out, g[n]["f"])
 
     def p3(n):
@@ -235,8 +226,8 @@
         wait(g[n]["f"], flr.at[s, us])
         mf[s, us, c, x] = mp[s, us, c, x] + flr[s, us, 0] + flr[s, us, 1]
         top, low, whole = mf.at[s, us, c, x, TOP], mf.at[s, us, c, x, LOW], mf.at[s, us, c, x]
-        send(top, top, x_right, g_right, g[n]["gr"])
-        send(low, low, x_left, g_left, g[n]["gl"])
+        send(top, top, x_right, g_right, g[n]["g1"])
+        send(low, low, x_left, g_left, g[n]["g1"])
         send(low, low, x_right, g_right, g[n]["g2"])
         send(top, top, x_left, g_left, g[n]["g2"])
         send(whole, whole, partner, q_out, g[n]["q"])
@@ -245,9 +236,8 @@
         s, us, _ = at(n)
         left, right = mf.at[s, us, c, xl], mf.at[s, us, c, xr]
         left_top, right_low = mf.at[s, us, c, xl, TOP], mf.at[s, us, c, xr, LOW]
-        wait(g[n]["gr"], left_top)
+        wait(g[n]["g1"], left)
         send(left_top, left_top, x_right, h_out, g[n]["h"])
-        wait(g[n]["gl"], right_low)
         send(right_low, right_low, x_left, h_out, g[n]["h"])
         wait(g[n]["g2"], left)
         send(left, left, partner, q_out, g[n]["q"])
@@ -276,63 +266,47 @@
             pacc[s, r] = part
             begun.add((s, r))
 
-    w = {(s, r): [recv() for _ in range(3)] for s in range(NS) for r in range(2)}
-    za_out, zb_out, z1_out, z0_out = sender(za, zb, zlr.at[:, :, 0], zlr.at[:, :, 0])
+    w = {(s, r): (recv(), recv()) for s in range(NS) for r in range(2)}
+    za_out, z1_out, z0_out = sender(zab, zlr.at[:, :, 0], zlr.at[:, :, 0])
 
     def z1(s, r):
-        a, b, f = w[s, r]
-        send(pacc.at[s, r, 3, LO], za.at[s, r], s_right, za_out, a)
-        send(pacc.at[s, r, 3, HI], zb.at[s, r], s_left, zb_out, b)
+        a, f = w[s, r]
+        send(pacc.at[s, r, 3, LO], zab.at[s, r, 0], s_right, za_out, a)
+        send(pacc.at[s, r, 3, HI], zab.at[s, r, 1], s_left, za_out, a)
         send(pacc.at[s, r, 2, HI], zlr.at[s, r, 0, HI], s_right, z1_out, f)
         send(pacc.at[s, r, 1, LO], zlr.at[s, r, 1, LO], s_left, z1_out, f)
 
     def z2(s, r):
-        a, b, f = w[s, r]
-        wait(a, za.at[s, r])
-        pacc[s, r, 2, LO] += za[s, r]
+        a, f = w[s, r]
+        wait(a, zab.at[s, r])
+        pacc[s, r, 2, LO] += zab[s, r, 0]
         send(pacc.at[s, r, 2, LO], zlr.at[s, r, 0, LO], s_right, z0_out, f)
-        wait(b, zb.at[s, r])
-        pacc[s, r, 1, HI] += zb[s, r]
+        pacc[s, r, 1, HI] += zab[s, r, 1]
         send(pacc.at[s, r, 1, HI], zlr.at[s, r, 1, HI], s_left, z0_out, f)
 
     parity = lax.rem(y, 2)
     t_core = lax.div(y, 2)
-    diagonal = x == z
+    apart = lax.rem(x - z + 4, 4)
+    diagonal, far = apart == 0, apart == 2
+    near = jnp.logical_or(apart == 1, apart == 3)
     stays = [jnp.logical_and(c == t_core, parity == r) for r in range(2)]
 
-    def t_send_to(s, r, src, to_x, to_z, sem):
-        return pltpu.make_async_remote_copy(
-            src_ref=src, dst_ref=tb.at[s, parity], send_sem=sem, recv_sem=t_recv.at[s],
-            device_id=(to_x, t_core, to_z, 2 * c + r), device_id_type=MESH,
-        )
-
     def t_first(s, r):
-        src = pf.at[s, r]
-        yield diagonal, stays[r], tb.at[s, parity], t_recv.at[s], (x, t_core, z, 2 * c + r)
-        if s in RELAYED:
-            k = RELAYED.index(s)
-            yield jnp.logical_not(diagonal), None, hop.at[k, r, z], hop_recv.at[k, r], dev(z=x)
+        end, in_plane = (tb.at[s, parity], t_recv.at[s]), (x, t_core, z, 2 * c + r)
+        yield diagonal, stays[r], *end, in_plane
+        yield far, None, hop.at[s, r], hop_recv.at[s, r], dev(z=x)
+        if s < TURNED:
+            yield near, stays[r], turn.at[s, parity], turn_recv.at[s], in_plane
         else:
-            k = s // 2
-            yield jnp.logical_not(diagonal), stays[r], turn.at[k, parity], turn_recv.at[k], (x, t_core, z, 2 * c + r)
+            yield near, None, *end, (z, t_core, x, 2 * c + r)
 
     def t_copy(s, r, dst, sem, to):
         return pltpu.make_async_remote_copy(
             src_ref=pf.at[s, r], dst_ref=dst, send_sem=t_send.at[s, r], recv_sem=sem, device_id=to, device_id_type=MESH,
         )
 
-    def t_second(s, r, d):
-        slot = lax.rem(x + d, 4)
-        return t_send_to(s, r, hop.at[RELAYED.index(s), r, slot], slot, x, hop_send.at[0])
-
-    def turned(s):
-        return pltpu.make_async_remote_copy(
-            src_ref=turn.at[s // 2], dst_ref=tb.at[s], send_sem=turn_send.at[0], recv_sem=t_recv.at[s],
-            device_id=dev(x=z, z=x), device_id_type=MESH,
-        )
-
     def z3(s, r):
-        wait(w[s, r][2], zlr.at[s, r])
+        wait(w[s, r][1], zlr.at[s, r])
         pf[s, r] = pacc[s, r, 0] + zlr[s, r, 0] + zlr[s, r, 1]
         for case, local_case, dst, sem, to in t_first(s, r):
             away = case if local_case is None else jnp.logical_and(case, jnp.logical_not(local_case))
@@ -348,17 +322,16 @@
                     pltpu.make_async_copy(pf.at[s, r], dst, sem).start()
 
     def pass_on(s):
-        @pl.when(jnp.logical_not(diagonal))
+        @pl.when(near)
         def _():
-            wait(turn_recv.at[s // 2], turn.at[s // 2])
-            turned(s).start()
+            wait(turn_recv.at[s], turn.at[s])
+            send(turn.at[s], tb.at[s], dev(x=z, z=x), turn_send.at[0], t_recv.at[s])
 
     def relay(s, r):
         @pl.when(diagonal)
         def _():
-            wait(hop_recv.at[RELAYED.index(s), r], hop.at[0, 0, three])
-            for d in range(1, 4):
-                t_second(s, r, d).start()
+            wait(hop_recv.at[s, r], hop.at[s, r])
+            send(hop.at[s, r], tb.at[s, parity], (xo, t_core, x, 2 * c + r), hop_send.at[0], t_recv.at[s])
 
     def turn_own():
         for n in range(2):
@@ -450,7 +423,7 @@
 
     load_h.wait()
     sums = [jnp.zeros((8, 128), F32) for _ in range(7)]
-    for s in (1, 0, 3, 2):
+    for s in range(NS):
         wait(t_recv.at[s], tb.at[s])
         for half in range(2):
             start = 256 * half + 64 * s
@@ -507,38 +480,37 @@
     for k in range(7):
         row = jnp.where(lane == k, weights[k], row)
     w_ref[...] = row
-    spread = [jnp.broadcast_to(v, (8, 128)) for v in weights]
 
     for r in range(2):
 
         def mix(n, carry):
-            part = pl.ds(pl.multiple_of(8 * n, 8), 8)
-            rows = pl.ds(pl.multiple_of(256 * r + 8 * n, 8), 8)
+            part = pl.ds(pl.multiple_of(32 * n, 32), 32)
+            rows = pl.ds(pl.multiple_of(256 * r + 32 * n, 32), 32)
             for col in range(2):
-                v = spread[6] * fg[0, r, col, part, :]
+                v = weights[6] * fg[0, r, col, part, :]
                 for k in range(6):
-                    v = v + spread[k] * fh[k, rows, lanes[col]]
+                    v = v + weights[k] * fh[k, rows, lanes[col]]
                 out[rows, lanes[col]] = v
             return carry
 
-        lax.fori_loop(0, 32, mix, 0)
+        lax.fori_loop(0, 8, mix, 0)
     for sem, ref in outgoing:
         wait(sem, ref)
     for s in range(NS):
         for r in range(2):
-            here = jnp.logical_and(diagonal, stays[r]) if s in RELAYED else stays[r]
+            here = jnp.logical_and(stays[r], jnp.logical_or(diagonal, near) if s < TURNED else diagonal)
 
             @pl.when(jnp.logical_not(here))
             def _():
                 wait(t_send.at[s, r], pf.at[s, r])
 
-    @pl.when(jnp.logical_not(diagonal))
+    @pl.when(near)
     def _():
         wait(turn_send.at[0], turn)
 
     @pl.when(diagonal)
     def _():
-        wait(hop_send.at[0], hop.at[:, :, three])
+        wait(hop_send.at[0], hop)
 
 
 def body(fock_matrix, density, basis_gram, error_history, fock_history):
@@ -557,14 +529,14 @@
             b(NS, 256, 512), b(NS, 256, 512), b(NU, 512, 256), b(NU, 512, 256),
             b(NU, 2, 256, 256), b(NU, 2, 256, 256),
             v(NS, NU, 2, 4, 32, 256), v(NS, NU, 4, 32, 256),
-            v(NS, NU, 16, 256), v(NS, NU, 16, 256), v(NS, NU, 2, 32, 256),
+            v(NS, NU, 2, 16, 256), v(NS, NU, 2, 32, 256),
             v(NS, NU, 2, 4, 32, 256), b(NS, NU, 256, 256), b(NS, NU, 256, 256),
-            v(NS, 2, 4, 64, 256), v(NS, 2, 32, 256), v(NS, 2, 32, 256), v(NS, 2, 2, 64, 256),
-            v(NS, 2, 64, 256), v(NS, 2, 64, 256), v(2, 2, 4, 64, 256), v(2, 2, 64, 256),
+            v(NS, 2, 4, 64, 256), v(NS, 2, 2, 32, 256), v(NS, 2, 2, 64, 256),
+            v(NS, 2, 64, 256), v(NS, 2, 64, 256), v(NS, 2, 64, 256), v(TURNED, 2, 64, 256),
             v(6, 512, 256), v(6, 512, 256), v(512, 256),
             v(16, 24, 128), v(8, 24, 128), v(16, 8, 128), v(8, 8, 128),
-            dma((20,)), dma((N_RECV,)), dma((9,)),
-            dma((NS, 2)), dma((NS,)), dma((2, 2)), dma((1,)), dma((2,)), dma((1,)),
+            dma((18,)), dma((N_RECV,)), dma((9,)),
+            dma((NS, 2)), dma((NS,)), dma((NS, 2)), dma((1,)), dma((TURNED,)), dma((1,)),
         ],
         compiler_params=pltpu.CompilerParams(
             collective_id=0, has_side_effects=True, vmem_limit_bytes=60 * 1024 * 1024

time: 98.4 us -> 95 us (0.965)
  Pallas kernels: 95.6 us -> 92.1 us
    pallas_call x1, Pallas kernels: 95.6 us -> 92.1 us  [body(): pl.pallas_call(kernel, out_shape=(block, block, pltpu.VMEM((1, 128), F32)...]
where the time goes in v4:
time: 95 us; the launch traced here: 94.9 us
  Pallas kernels  92.1 us (97%)
  local copies, waits for them, and re-layouts  2.1 us (2%)
    pallas_call x1, Pallas kernels, body(): pl.pallas_call(kernel, out_shape=(block, block, pltpu.VMEM((1, 128), F32)...  92.1 us

profile of v4, /device:TPU:1, one launch (start us, length us, event | category | flops | bytes accessed | tf_op | source)
XLA Modules:
  0.0 94.9 jit_solution(17772156161028053812)
XLA Ops:
  0.6 92.1 %shard_map.76 = (f32[512,256]{1,0:T(8,128)S(1)}, f32[512,256]{1,0:T(8,128)S(1)}, f32[1,128]{1,0:T(1,128)S(1)}) custom-call(f32[512,256]{1,0:T(8,128)} %f_hbm.1, f32[512,256]{1,0:T(8,128)} %d_hbm.1, f32[512,256]{1,0:T(8,128)} %s_hbm.1, f32[6,512,256]{2,1,0:T(8,128)} %eh_hbm.1, f32[6,512,256]{2,1,0:T(8,128)} %fh_hbm.1), custom_call_target="tpu_custom_call" | custom-call | tf_op jit(solution)/shard_map/pallas_call | solution.py:522
  92.8 0.8 copy.10
  93.6 0.5 slice_bitcast_fusion
  94.1 0.8 copy.11

commit v5 on v4

--- a/solution.py
+++ b/solution.py
@@ -17,27 +17,27 @@
     (3, 3, 1),
 )
 ORDER = (
-    ("ys", 0), ("zs", 0), ("zs", 1), ("zf", 0), ("zf", 1), ("zs", 3), ("yf", 0), ("pd", 0), ("zs", 2), ("fs", 0),
-    ("pd", 1), ("ps", 0), ("p0", 1), ("p0", 0), ("ps", 1), ("p0", 2), ("p1", 1), ("p1", 0), ("p1", 2), ("hist", 0),
-    ("zf", 3), ("p2", 1), ("pd", 2), ("p2", 0), ("p0", 3), ("zf", 2), ("p2", 2), ("p1", 3), ("p3", 1), ("p3", 0),
-    ("p3", 2), ("pd", 3), ("p0", 4), ("p0", 5), ("p2", 3), ("p4", 1), ("p1", 4), ("ps", 2), ("p4", 0), ("ps", 3),
-    ("pf", 0, 0), ("p1", 5), ("p0", 7), ("ff", 0), ("p3", 3), ("p2", 4), ("p1", 7), ("p0", 6), ("fs", 1), ("p2", 5),
-    ("p4", 2), ("p4", 3), ("p3", 4), ("p0", 10), ("p5", 0), ("p1", 6), ("p0", 9), ("p5", 1), ("pf", 1, 0), ("p3", 5),
-    ("p6", 1, 0), ("p0", 8), ("p4", 4), ("p1", 9), ("p2", 7), ("p5", 3), ("ff", 1), ("pf", 0, 1), ("pf", 1, 1),
-    ("pf", 3, 0), ("p6", 0, 0), ("p1", 10), ("p2", 6), ("pf", 2, 0), ("p4", 5), ("p5", 2), ("p1", 8), ("p5", 4),
-    ("p6", 3, 0), ("p6", 4, 0), ("z1", 0, 0), ("p6", 0, 1), ("pf", 2, 1), ("p3", 7), ("p6", 1, 1), ("p2", 9),
-    ("p6", 3, 1), ("pf", 3, 1), ("p6", 4, 1), ("z1", 0, 1), ("p3", 6), ("p5", 5), ("p2", 10), ("p6", 2, 0),
-    ("p6", 2, 1), ("z2", 0, 0), ("p6", 5, 0), ("z1", 1, 0), ("p2", 8), ("p4", 7), ("p3", 9), ("z2", 0, 1),
-    ("p6", 5, 1), ("z1", 1, 1), ("p4", 6), ("p3", 10), ("z2", 1, 0), ("p3", 8), ("z3", 0, 0), ("p5", 7), ("z3", 0, 1),
-    ("ha",), ("p4", 9), ("z2", 1, 1), ("p5", 6), ("p6", 7, 0), ("p6", 7, 1), ("p4", 10), ("z3", 1, 0), ("p6", 6, 0),
-    ("p6", 6, 1), ("p4", 8), ("z1", 2, 1), ("p5", 9), ("z3", 1, 1), ("z1", 2, 0), ("p5", 10), ("p6", 9, 0), ("p5", 8),
-    ("p6", 10, 0), ("z2", 2, 1), ("p6", 10, 1), ("p6", 8, 0), ("z1", 3, 0), ("p6", 9, 1), ("u", 1), ("z2", 2, 0),
-    ("p6", 8, 1), ("z1", 3, 1), ("t", 1, 1), ("u", 0), ("z2", 3, 0), ("z3", 2, 1), ("t", 0, 1), ("z2", 3, 1),
-    ("t", 1, 0), ("z3", 2, 0), ("z3", 3, 0), ("t", 0, 0), ("z3", 3, 1), ("own",), ("t", 2, 1), ("t", 2, 0), ("u", 2),
-    ("t", 3, 0), ("t", 3, 1), ("hb",),
+    ("ys", 0), ("zs", 1), ("zs", 0), ("zf", 1), ("zf", 0), ("yf", 0), ("pd", 1), ("pd", 0), ("ps", 1), ("p0", 2),
+    ("zs", 2), ("ps", 0), ("p0", 0), ("fs", 0), ("p1", 2), ("p1", 0), ("p0", 1), ("p2", 2), ("pd", 2), ("zf", 2),
+    ("p1", 1), ("p0", 3), ("p2", 0), ("p1", 3), ("p3", 2), ("p2", 1), ("pd", 3), ("p3", 0), ("p0", 4), ("p0", 5),
+    ("p2", 3), ("zs", 3), ("p1", 4), ("ps", 2), ("p1", 5), ("p0", 7), ("ff", 0), ("p3", 1), ("pf", 1, 0), ("p3", 3),
+    ("p2", 4), ("zf", 3), ("p2", 5), ("p4", 0), ("fs", 1), ("p4", 2), ("hist", 0), ("pf", 2, 0), ("p4", 1), ("p0", 6),
+    ("p4", 3), ("pf", 0, 0), ("p3", 4), ("p1", 7), ("ps", 3), ("p0", 8), ("p0", 9), ("p5", 2), ("p5", 0), ("p3", 5),
+    ("p0", 10), ("pf", 0, 1), ("p4", 4), ("p5", 1), ("p1", 6), ("p6", 2, 0), ("p5", 3), ("pf", 3, 0), ("ff", 1),
+    ("p6", 0, 0), ("pf", 1, 1), ("p2", 7), ("p6", 1, 0), ("p6", 3, 0), ("p6", 2, 1), ("p4", 5), ("p5", 4), ("p1", 8),
+    ("pf", 2, 1), ("p6", 4, 0), ("p2", 6), ("z1", 0, 0), ("p6", 0, 1), ("p1", 9), ("p6", 3, 1), ("p6", 1, 1),
+    ("p1", 10), ("pf", 3, 1), ("p5", 5), ("p6", 4, 1), ("z1", 0, 1), ("p3", 7), ("p6", 5, 0), ("z1", 1, 0), ("p3", 6),
+    ("z2", 0, 0), ("p2", 9), ("p2", 8), ("z2", 0, 1), ("p2", 10), ("p6", 5, 1), ("z1", 1, 1), ("p4", 7), ("z2", 1, 0),
+    ("p4", 6), ("z3", 0, 0), ("p3", 9), ("z3", 0, 1), ("ha",), ("p3", 8), ("p5", 7), ("p3", 10), ("z2", 1, 1),
+    ("p5", 6), ("z3", 1, 0), ("p6", 7, 0), ("p4", 9), ("p6", 6, 0), ("z1", 2, 0), ("p6", 6, 1), ("p4", 8),
+    ("p6", 7, 1), ("z1", 2, 1), ("p4", 10), ("p5", 9), ("z3", 1, 1), ("p5", 8), ("t", 0, 1), ("p6", 9, 0), ("p5", 10),
+    ("z2", 2, 0), ("z2", 2, 1), ("p6", 8, 0), ("p6", 10, 0), ("z1", 3, 0), ("p6", 9, 1), ("p6", 8, 1), ("p6", 10, 1),
+    ("z1", 3, 1), ("t", 0, 0), ("z2", 3, 0), ("t", 1, 1), ("z3", 2, 0), ("z2", 3, 1), ("z3", 2, 1), ("u", 1),
+    ("z3", 3, 0), ("t", 1, 0), ("z3", 3, 1), ("own",), ("t", 2, 0), ("u", 0), ("t", 2, 1), ("t", 3, 0),
+    ("t", 3, 1), ("hb",),
 )
 N_RECV = 41 + 7 * len(GROUPS)
-TURNED = 3
+TURNED = 2
 
 
 def split(v):

time: 95 us -> 95.8 us (level)
  no operation moved by 1% of the time
where the time goes in v5:
time: 95.8 us; the launch traced here: 95.7 us
  Pallas kernels  93 us (97%)
  local copies, waits for them, and re-layouts  2.1 us (2%)
    pallas_call x1, Pallas kernels, body(): pl.pallas_call(kernel, out_shape=(block, block, pltpu.VMEM((1, 128), F32)...  93 us

profile of v5, /device:TPU:1, one launch (start us, length us, event | category | flops | bytes accessed | tf_op | source)
XLA Modules:
  0.0 95.7 jit_solution(16732325143302863318)
XLA Ops:
  0.6 93.0 %shard_map.76 = (f32[512,256]{1,0:T(8,128)S(1)}, f32[512,256]{1,0:T(8,128)S(1)}, f32[1,128]{1,0:T(1,128)S(1)}) custom-call(f32[512,256]{1,0:T(8,128)} %f_hbm.1, f32[512,256]{1,0:T(8,128)} %d_hbm.1, f32[512,256]{1,0:T(8,128)} %s_hbm.1, f32[6,512,256]{2,1,0:T(8,128)} %eh_hbm.1, f32[6,512,256]{2,1,0:T(8,128)} %fh_hbm.1), custom_call_target="tpu_custom_call" | custom-call | tf_op jit(solution)/shard_map/pallas_call | solution.py:522
  93.6 0.8 copy.10
  94.4 0.5 slice_bitcast_fusion
  94.9 0.8 copy.11

commit v6 on v4

--- a/solution.py
+++ b/solution.py
@@ -89,13 +89,10 @@
     def wait(sem, ref):
         pltpu.make_async_copy(ref, ref, sem).wait()
 
-    local = []
-
-    def load(src, dst):
-        copy = pltpu.make_async_copy(src, dst, local_sem.at[len(local)])
-        copy.start()
-        local.append(copy)
-        return copy
+    def load(k, *pairs):
+        for src, dst in pairs:
+            pltpu.make_async_copy(src, dst, local_sem.at[k]).start()
+
 
     lanes = [pl.ds(0, 128), pl.ds(128, 128)]
     halves = [pl.ds(0, 256), pl.ds(256, 256)]
@@ -103,12 +100,12 @@
     barrier = pltpu.get_barrier_semaphore()
     for to in (x_right, x_left, d_right, d_left, s_right, s_left, partner):
         pl.semaphore_signal(barrier, inc=1, device_id=to, device_id_type=MESH)
-    load_s = load(s_hbm, s_in)
-    load_d = [load(d_hbm.at[:, lanes[h]], dg.at[0, h]) for h in range(2)]
-    load_e = load(eh_hbm, eh)
-    load_f = [load(f_hbm.at[halves[r], lanes[h]], fg.at[0, r, h]) for r in range(2) for h in range(2)]
-    load_h = load(fh_hbm, fh)
-    load_s.wait()
+    load(0, (s_hbm, s_in))
+    load(1, *((d_hbm.at[:, lanes[h]], dg.at[0, h]) for h in range(2)))
+    load(2, (eh_hbm, eh))
+    load(3, *((f_hbm.at[halves[r], lanes[h]], fg.at[0, r, h]) for r in range(2) for h in range(2)))
+    load(4, (fh_hbm, fh))
+    wait(local_sem.at[0], s_in)
     for n in range(2):
         for k in range(4):
             block = s_in[pl.ds(128 * k, 128), lanes[n]].T
@@ -381,7 +378,7 @@
     hist = []
 
     def first_gram():
-        load_e.wait()
+        wait(local_sem.at[2], eh)
         hist.extend(history_gram() + [jnp.zeros((3, 128), F32)])
 
     def do_ps(s):
@@ -391,8 +388,7 @@
 
     def do_pd(u):
         if u == 0:
-            for copy in load_d:
-                copy.wait()
+            wait(local_sem.at[1], dg.at[0])
         if u == 2:
             d_line.second()
         if u == 3:
@@ -401,8 +397,7 @@
 
     def do_pf(u, r):
         if u == 0 and r == 0:
-            for copy in load_f:
-                copy.wait()
+            wait(local_sem.at[3], fg.at[0])
         if u == 2:
             f_line[r].second()
         if u == 3:
@@ -421,7 +416,7 @@
     for phase, *where in ORDER:
         work[phase](*where)
 
-    load_h.wait()
+    wait(local_sem.at[4], fh)
     sums = [jnp.zeros((8, 128), F32) for _ in range(7)]
     for s in range(NS):
         wait(t_recv.at[s], tb.at[s])
@@ -429,14 +424,15 @@
             start = 256 * half + 64 * s
 
             def step(n, acc):
-                rows = pl.ds(pl.multiple_of(start + 8 * n, 8), 8)
+                rows = pl.ds(pl.multiple_of(start + 32 * n, 32), 32)
                 for col in range(2):
-                    e = own[rows, lanes[col]] - tb[s, half, pl.ds(pl.multiple_of(8 * n, 8), 8), lanes[col]]
+                    e = own[rows, lanes[col]] - tb[s, half, pl.ds(pl.multiple_of(32 * n, 32), 32), lanes[col]]
                     err[rows, lanes[col]] = e
-                    acc = tuple(acc[k] + eh[k, rows, lanes[col]] * e for k in range(6)) + (acc[6] + e * e,)
+                    terms = [eh[k, rows, lanes[col]] * e for k in range(6)] + [e * e]
+                    acc = tuple(v + jnp.sum(t.reshape(4, 8, 128), axis=0) for v, t in zip(acc, terms))
                 return acc
 
-            sums = lax.fori_loop(0, 8, step, tuple(sums))
+            sums = lax.fori_loop(0, 2, step, tuple(sums))
 
     sum_plane(1, na, [jnp.sum(v, axis=0, keepdims=True) for v in sums] + [jnp.zeros((1, 128), F32)])
     sum_line(1, nb, na)
@@ -535,7 +531,7 @@
             v(NS, 2, 64, 256), v(NS, 2, 64, 256), v(NS, 2, 64, 256), v(TURNED, 2, 64, 256),
             v(6, 512, 256), v(6, 512, 256), v(512, 256),
             v(16, 24, 128), v(8, 24, 128), v(16, 8, 128), v(8, 8, 128),
-            dma((18,)), dma((N_RECV,)), dma((9,)),
+            dma((18,)), dma((N_RECV,)), dma((5,)),
             dma((NS, 2)), dma((NS,)), dma((NS, 2)), dma((1,)), dma((TURNED,)), dma((1,)),
         ],
         compiler_params=pltpu.CompilerParams(

time: 95 us -> 94.8 us (level)
  no operation moved by 1% of the time
where the time goes in v6:
time: 94.8 us; the launch traced here: 94.7 us
  Pallas kernels  91.9 us (97%)
  local copies, waits for them, and re-layouts  2.1 us (2%)
    pallas_call x1, Pallas kernels, body(): pl.pallas_call(kernel, out_shape=(block, block, pltpu.VMEM((1, 128), F32)...  91.9 us

profile of v6, /device:TPU:1, one launch (start us, length us, event | category | flops | bytes accessed | tf_op | source)
XLA Modules:
  0.0 94.7 jit_solution(4050073470659926135)
XLA Ops:
  0.6 91.9 %shard_map.76 = (f32[512,256]{1,0:T(8,128)S(1)}, f32[512,256]{1,0:T(8,128)S(1)}, f32[1,128]{1,0:T(1,128)S(1)}) custom-call(f32[512,256]{1,0:T(8,128)} %f_hbm.1, f32[512,256]{1,0:T(8,128)} %d_hbm.1, f32[512,256]{1,0:T(8,128)} %s_hbm.1, f32[6,512,256]{2,1,0:T(8,128)} %eh_hbm.1, f32[6,512,256]{2,1,0:T(8,128)} %fh_hbm.1), custom_call_target="tpu_custom_call" | custom-call | tf_op jit(solution)/shard_map/pallas_call | solution.py:518
  92.6 0.8 copy.10
  93.4 0.5 slice_bitcast_fusion
  93.9 0.8 copy.11
